TPU v7x, 256 devices: a 2x2x32 block of a 4x8x32 slice. The times are simulated.
256 devices in a mesh: groups: 4 (over y, x), expert: 64 (over z, core).
Axes of the slice: x: 2, y: 2, z: 32, core: 2. Of those that a mesh axis runs over, the one named last changes fastest.
The devices are a block of a 4x8x32 slice.
Arguments:
- queries: bfloat16 [2048, 4096], P(('groups', 'expert')), parts along dimension 0, may hold values from -150 to 150
- key_cache: bfloat16 [2048, 64, 512], P(('groups', 'expert')), parts along dimension 0, may hold values from -7 to 7
- value_cache: bfloat16 [2048, 64, 512], P(('groups', 'expert')), parts along dimension 0, may hold values from -6 to 6
- new_key: bfloat16 [2048, 512], P(('groups', 'expert')), parts along dimension 0, may hold values from -6 to 6
- new_value: bfloat16 [2048, 512], P(('groups', 'expert')), parts along dimension 0, may hold values from -6 to 6
- cache_lengths: int32 [2048], P(('groups', 'expert')), parts along dimension 0, may hold values from 2 to 64, as said below
- hidden_in: bfloat16 [16384, 2048], P(('groups', 'expert')), parts along dimension 0, may hold values from -6 to 6
- norm_gain: bfloat16 [2048], replicated, may hold values from 0.5 to 1.5
- router_weight: bfloat16 [2048, 64], replicated, may hold values from -0.125 to 0.125
- expert_ids: int32 [16384, 8], P(('groups', 'expert')), parts along dimension 0, may hold values from 0 to 63, all different within a row; in each aligned block of 64 rows (0 to 63, 64 to 127, ...) at most 16 rows name the same one
- gate_train: bfloat16 [64, 2048, 768], P(None, 'expert'), may hold values from -0.125 to 0.125
- up_train: bfloat16 [64, 2048, 768], P(None, 'expert'), may hold values from -0.125 to 0.125
- down_train: bfloat16 [64, 768, 2048], P(None, 'expert'), may hold values from -0.21875 to 0.21875
Outputs:
- attended: bfloat16 [2048, 4096], P(('groups', 'expert')), parts along dimension 0
- expert_mix: bfloat16 [16384, 2048], P(('groups', 'expert')), parts along dimension 0
There are 4 independent parts, one for each index of `groups`. A program takes and returns all parts, laid end to end along the dimension named above; an argument that names none is the same for every part. Nothing has to cross between parts.
Inputs may be any that keep to these rules, and one draw needn't show every extreme that they name: `expert_ids`: each row names 8 different experts; within the rows of one device no expert is named more than 16 times. `cache_lengths`: the first sequence of each device's 8 has all 64 positions filled.
All inputs are finite; a program needn't handle non-finite values.
Results may differ from a plain program's by a relative error of at most 0.0074.
Values may be sent and summed in bfloat16 or wider, within the bound.
A program may use at most 128 MiB of HBM per device.

v0:
```python
import math

import jax
import jax.numpy as jnp
from jax import lax
from jax.sharding import Mesh
from jax.sharding import PartitionSpec as P

HEADS = 32
KV_HEADS = 4
HEAD_DIM = 128
CTX = 64
EXPERT = ("expert_0", "expert_1")
GROUPS_EXPERT = ("groups", "expert_0", "expert_1")


EPSILON = 1e-06


def side_by_side(arrays, axis, split_dim, concat_dim, along):
    widths = [a.shape[along] for a in arrays]
    both = jnp.concatenate(arrays, axis=along)
    whole = lax.all_to_all(both, axis, split_axis=split_dim, concat_axis=concat_dim, tiled=True)
    return tuple(jnp.split(whole, [sum(widths[:k]) for k in range(1, len(widths))], axis=along))


def split_up(x, dim, peers):
    dims = x.shape
    tiles = x.reshape(*dims[:dim], peers, dims[dim] // peers, *dims[dim + 1 :])
    return jnp.moveaxis(tiles, dim, 0)


def in_order(tiles, dim):
    tiles = jnp.moveaxis(tiles, 0, dim)
    dims = tiles.shape
    return tiles.reshape(*dims[:dim], dims[dim] * dims[dim + 1], *dims[dim + 2 :])


def turned_blocks(tiles, axes, turns):
    dims = [lax.axis_size(a) for a in axes]
    tiles = tiles.reshape(*dims, *tiles.shape[1:])
    for k in turns:
        tiles = lax.all_to_all(tiles, axes[k], split_axis=k, concat_axis=k, tiled=True)
    return tiles.reshape(-1, *tiles.shape[len(axes) :])


def exchange_by_chip(x, groups, turns, split_dim, concat_dim):
    peers = lax.axis_size(groups[0]) * lax.axis_size(groups[1])
    tiles = split_up(x, split_dim, peers)
    return in_order(turned_blocks(tiles, groups, turns), concat_dim)


def rms_normed(hidden_in, norm_gain):
    values = hidden_in.astype(jnp.float32)
    mean_square = jnp.mean(values * values, axis=-1, keepdims=True)
    return (values * lax.rsqrt(mean_square + EPSILON) * norm_gain.astype(jnp.float32)).astype(
        jnp.bfloat16
    )


def attend(queries, key_cache, value_cache, new_key, new_value, cache_lengths):
    seq_count = queries.shape[0]
    group_size = HEADS // KV_HEADS
    query_blocks = queries.reshape(seq_count, KV_HEADS, group_size, HEAD_DIM)
    cached_keys = key_cache.reshape(seq_count, CTX, KV_HEADS, HEAD_DIM)
    cached_values = value_cache.reshape(seq_count, CTX, KV_HEADS, HEAD_DIM)
    fresh_keys = new_key.reshape(seq_count, KV_HEADS, HEAD_DIM)
    fresh_values = new_value.astype(jnp.float32).reshape(seq_count, KV_HEADS, HEAD_DIM)
    score_scale = 1.0 / math.sqrt(HEAD_DIM)
    scores = (
        jnp.einsum("sgrd,scgd->sgrc", query_blocks, cached_keys, preferred_element_type=jnp.float32)
        * score_scale
    )
    own_score = (
        jnp.einsum("sgrd,sgd->sgr", query_blocks, fresh_keys, preferred_element_type=jnp.float32)
        * score_scale
    )
    positions = jnp.arange(CTX, dtype=jnp.int32)
    visible = positions[None, :] < cache_lengths[:, None]
    scores = jnp.where(visible[:, None, None, :], scores, -1e30)
    largest = jnp.maximum(jnp.max(scores, axis=-1), own_score)
    cached_exp = jnp.exp(scores - largest[..., None])
    own_exp = jnp.exp(own_score - largest)
    prob_total = jnp.sum(cached_exp, axis=-1) + own_exp
    cached_prob = (cached_exp / prob_total[..., None]).astype(jnp.bfloat16)
    own_prob = (own_exp / prob_total).astype(jnp.bfloat16).astype(jnp.float32)
    context = jnp.einsum(
        "sgrc,scgd->sgrd", cached_prob, cached_values, preferred_element_type=jnp.float32
    )
    context = context + own_prob[..., None] * fresh_values[:, :, None, :]
    return context.reshape(seq_count, HEADS * HEAD_DIM).astype(jnp.bfloat16)


def expert_rows(received, gate_weight, up_weight, down_weight):
    token_rows = received.reshape(-1, received.shape[2])
    gate_proj = jnp.dot(token_rows, gate_weight, preferred_element_type=jnp.float32)
    up_proj = jnp.dot(token_rows, up_weight, preferred_element_type=jnp.float32)
    hidden_units = (jax.nn.silu(gate_proj) * up_proj).astype(jnp.bfloat16)
    expert_out = jnp.dot(hidden_units, down_weight, preferred_element_type=jnp.float32).astype(
        jnp.bfloat16
    )
    return lax.all_to_all(
        expert_out.reshape(received.shape), EXPERT, split_axis=0, concat_axis=0, tiled=True
    )


def local(
    queries,
    key_cache,
    value_cache,
    new_key,
    new_value,
    cache_lengths,
    hidden_in,
    norm_gain,
    router_weight,
    expert_ids,
    gate_train,
    up_train,
    down_train,
):
    gate_moved, up_moved = side_by_side((gate_train, up_train), EXPERT, 0, 1, 2)
    attended = attend(queries, key_cache, value_cache, new_key, new_value, cache_lengths)
    tok_count = hidden_in.shape[0]
    expert_count = router_weight.shape[1]
    top_count = expert_ids.shape[1]
    width = hidden_in.shape[1]
    slot_count = 2 * tok_count * top_count // expert_count
    normed = rms_normed(hidden_in, norm_gain)
    logits = jnp.dot(normed, router_weight, preferred_element_type=jnp.float32)
    expert_range = jnp.arange(expert_count, dtype=jnp.int32)
    picked = expert_ids[:, :, None] == expert_range[None, None, :]
    chosen = jnp.sum(jnp.where(picked, logits[:, None, :], 0.0), axis=-1)
    mixing = jax.nn.softmax(chosen, axis=-1)
    onehot_int = picked.astype(jnp.int32).reshape(-1, expert_count)
    rank_values = jnp.sum((jnp.cumsum(onehot_int, axis=0) - 1) * onehot_int, axis=-1)
    targets = expert_ids.reshape(-1) * slot_count + rank_values
    slot_range = jnp.arange(expert_count * slot_count, dtype=jnp.int32)
    placing = slot_range[:, None] == targets[None, :]
    down_moved = exchange_by_chip(down_train, ("expert_0", "expert_1"), (1, 0), 0, 1)
    all_rows, all_ids = (
        lax.all_gather(normed, EXPERT, axis=0, tiled=True),
        lax.all_gather(expert_ids, EXPERT, axis=0, tiled=True),
    )
    device_count = lax.axis_size(EXPERT)
    own_index = lax.axis_index(EXPERT)
    own_hits = (all_ids == own_index).astype(jnp.int32).reshape(device_count, tok_count * top_count)
    own_ranks = jnp.cumsum(own_hits, axis=1) - 1
    own_targets = jnp.where(own_hits > 0, own_ranks, -1)
    token_owner = jnp.arange(tok_count * top_count, dtype=jnp.int32) // top_count
    slot_steps = jnp.arange(slot_count, dtype=jnp.int32)
    matches = own_targets[:, None, :] == slot_steps[None, :, None]
    local_token = jnp.sum(jnp.where(matches, token_owner[None, None, :], 0), axis=-1)
    filled = jnp.any(matches, axis=-1)
    row_index = jnp.arange(device_count, dtype=jnp.int32)[:, None] * tok_count + local_token
    taken = jnp.take(all_rows, row_index.reshape(-1), axis=0).reshape(
        device_count, slot_count, width
    )
    received = jnp.where(filled[..., None], taken, jnp.zeros_like(taken))
    returned = expert_rows(received, gate_moved[0], up_moved[0], down_moved[0])
    flat_back = returned.reshape(expert_count * slot_count, width)
    per_assign = lax.dot_general(
        placing.astype(jnp.bfloat16),
        flat_back,
        (((0,), (0,)), ((), ())),
        preferred_element_type=jnp.float32,
    )
    mixed_out = jnp.sum(
        mixing[:, :, None] * per_assign.reshape(tok_count, top_count, width), axis=1
    ).astype(jnp.bfloat16)
    return (attended, mixed_out)


def solution(mesh):
    torus = Mesh(
        mesh.devices.reshape(mesh.shape["groups"], 32, 2), ("groups", "expert_0", "expert_1")
    )
    placed = (
        P(GROUPS_EXPERT, None),
        P(GROUPS_EXPERT, None, None),
        P(GROUPS_EXPERT, None, None),
        P(GROUPS_EXPERT, None),
        P(GROUPS_EXPERT, None),
        P(GROUPS_EXPERT),
        P(GROUPS_EXPERT, None),
        P(),
        P(),
        P(GROUPS_EXPERT, None),
        P(None, EXPERT, None),
        P(None, EXPERT, None),
        P(None, EXPERT, None),
    )
    return jax.shard_map(
        local,
        mesh=torus,
        in_specs=placed,
        out_specs=(P(GROUPS_EXPERT, None), P(GROUPS_EXPERT, None)),
        check_vma=False,
    )
```

profile of v0, /device:TPU:38, one launch (start us, length us, event | category | flops | bytes accessed | tf_op | source)
XLA Modules:
  0.0 1476.7 jit_solution(11159508898788602828)
XLA Ops:
  7.2 6.1 reshape_reshape.3
  13.3 3.3 copy.82
  16.5 6.3 all_to_all.27
  22.8 4.9 copy.83
  27.7 32.7 %all-to-all-start.2 = ((bf16[32,2,1,12,2048]{4,1,3,2,0:T(2,128)(2,1)}), bf16[32,2,1,12,2048]{4,1,3,2,0:T(2,128)(2,1)}, u32[]{:S(2)}, u32[]{:S(2)}) async-start(bf16[32,2,1,12,2048]{4,1,3,2,0:T(2,128)(2,1)} %copy.83), calls=%async_computation.2 | async-start | bytes 6291456 | tf_op jit(solution)/shard_map/all_to_all | solution.py:43
  60.4 6.2 pad_maximum_fusion
  66.6 269.7 %all-to-all-done.2 = bf16[32,2,1,12,2048]{4,1,3,2,0:T(2,128)(2,1)} async-done(((bf16[32,2,1,12,2048]{4,1,3,2,0:T(2,128)(2,1)}), bf16[32,2,1,12,2048]{4,1,3,2,0:T(2,128)(2,1)}, u32[]{:S(2)}, u32[]{:S(2)}) %all-to-all-start.2) | async-done | bytes 3145760 | tf_op jit(solution)/shard_map/all_to_all | solution.py:43
  336.2 18.8 %all-to-all-start = ((bf16[64,32,1536]{2,1,0:T(8,128)(2,1)}), bf16[64,32,1536]{2,1,0:T(8,128)(2,1)}, u32[]{:S(2)}, u32[]{:S(2)}) async-start(bf16[64,32,1536]{2,1,0:T(8,128)(2,1)} %pad_maximum_fusion), calls=%async_computation | async-start | bytes 12582912 | tf_op jit(solution)/shard_map/all_to_all | solution.py:23
  355.2 0.2 fusion.9
  355.4 0.8 fusion.11
  356.3 652.4 %all-gather = s32[64,64,8]{1,2,0:T(8,128)S(1)} all-gather(s32[1,64,8]{1,2,0:T(8,128)S(1)} %bitcast.86), channel_id=1, replica_groups=mesh['groups'=4,'expert_0'=32,'expert_1'=2] {'expert_0','expert_1'}, dimensions={0}, use_global_device_ids=true | all-gather | bytes 133120 | tf_op jit(solution)/shard_map/all_gather | solution.py:143
  1008.7 0.2 copy.76
  1008.9 0.2 copy.77
  1009.0 0.1 copy.78
  1009.2 1.2 reduce-window.16
  1010.4 0.2 slice_reduce_fusion
  1010.6 0.1 add_add_fusion
  1010.8 0.1 copy.87
  1010.9 0.1 copy.81
  1011.1 1.2 select_reduce_fusion
  1012.3 0.1 add.105
  1012.4 0.1 add.102
  1012.5 1.2 fusion.2
  1013.7 0.1 broadcast_in_dim.86
  1013.8 5.4 copy.84
  1019.2 6.2 squeeze_reshape_transpose_reshape.3
  1025.4 16.7 %gather_fusion = bf16[1024,2048]{1,0:T(8,128)(2,1)} fusion(bf16[4096,2048]{1,0:T(8,128)(2,1)} %all-gather.3.cloned.1.call-done, s32[1024]{0:T(1024)S(1)} %broadcast_clamp_fusion), kind=kCustom, calls=%fused_computation | custom fusion | bytes 8392704 | tf_op jit(solution)/shard_map/jit(_take)/gather | solution.py:156
  1042.1 8.3 fusion
  1050.5 13.7 convolution_convert_fusion
  1064.2 20.8 %all-to-all-start.3 = ((bf16[64,16,2048]{2,1,0:T(8,128)(2,1)}), bf16[64,16,2048]{2,1,0:T(8,128)(2,1)}, u32[]{:S(2)}, u32[]{:S(2)}) async-start(bf16[64,16,2048]{2,1,0:T(8,128)(2,1)} %bitcast.79), calls=%async_computation.3 | async-start | bytes 8388608 | tf_op jit(solution)/shard_map/all_to_all | solution.py:102
  1085.0 0.1 copy.72
  1085.1 0.1 reshape.276
  1085.2 0.1 eq.78
  1085.3 1.2 reduce-window.14
  1086.5 0.2 slice_reduce_fusion.1
  1086.9 0.2 fusion.22
  1087.0 0.5 fusion.34
  1087.5 0.2 fusion.19
  1087.8 0.3 fusion.7
  1088.1 0.7 copy.113
  1088.8 0.2 fusion.35
  1089.0 0.2 select_reduce_fusion.1
  1089.2 0.1 reduce_max.19
  1089.3 0.2 fusion.26
  1089.5 0.1 fusion.17
  1089.7 0.1 fusion.25
  1089.8 374.1 %all-to-all-done.3 = bf16[64,16,2048]{2,1,0:T(8,128)(2,1)} async-done(((bf16[64,16,2048]{2,1,0:T(8,128)(2,1)}), bf16[64,16,2048]{2,1,0:T(8,128)(2,1)}, u32[]{:S(2)}, u32[]{:S(2)}) %all-to-all-start.3) | async-done | bytes 4194336 | tf_op jit(solution)/shard_map/all_to_all | solution.py:102
  1463.9 6.0 multiply_reduce_fusion
  (47 shorter events, 0.6 us)
Async XLA Ops:
  7.2 1080.6 %copy-start = (bf16[8,64,512]{2,1,0:T(8,128)(2,1)S(1)}, bf16[8,64,512]{2,1,0:T(8,128)(2,1)}, u32[]{:S(2)}) copy-start(bf16[8,64,512]{2,1,0:T(8,128)(2,1)} %param.15) | copy-start | bytes 1572868
  27.7 308.5 %all-to-all-start.2 = ((bf16[32,2,1,12,2048]{4,1,3,2,0:T(2,128)(2,1)}), bf16[32,2,1,12,2048]{4,1,3,2,0:T(2,128)(2,1)}, u32[]{:S(2)}, u32[]{:S(2)}) async-start(bf16[32,2,1,12,2048]{4,1,3,2,0:T(2,128)(2,1)} %copy.83), calls=%async_computation.2 | async-start | bytes 6291456 | tf_op jit(solution)/shard_map/all_to_all | solution.py:43
  66.6 288.6 %copy-start.8 = (bf16[2048]{0:T(1024)(128)(2,1)S(1)}, bf16[2048]{0:T(1024)(128)(2,1)}, u32[]{:S(2)}) copy-start(bf16[2048]{0:T(1024)(128)(2,1)} %param.20) | copy-start | bytes 12292
  66.6 288.6 %copy-start.2 = (bf16[64,2048]{1,0:T(8,128)(2,1)S(1)}, bf16[64,2048]{1,0:T(8,128)(2,1)}, u32[]{:S(2)}) copy-start(bf16[64,2048]{1,0:T(8,128)(2,1)} %param.19) | copy-start | bytes 786436
  66.6 289.7 %copy-start.6 = (s32[64,8]{0,1:T(8,128)S(1)}, s32[64,8]{0,1:T(8,128)}, u32[]{:S(2)}) copy-start(s32[64,8]{0,1:T(8,128)} %param.22) | copy-start | bytes 6148
  336.2 705.9 %all-to-all-start = ((bf16[64,32,1536]{2,1,0:T(8,128)(2,1)}), bf16[64,32,1536]{2,1,0:T(8,128)(2,1)}, u32[]{:S(2)}, u32[]{:S(2)}) async-start(bf16[64,32,1536]{2,1,0:T(8,128)(2,1)} %pad_maximum_fusion), calls=%async_computation | async-start | bytes 12582912 | tf_op jit(solution)/shard_map/all_to_all | solution.py:23
  355.1 670.3 %all-gather.3.cloned.1.call-start = ((), (), s32[]{:S(2)}) async-start(), calls=%async_computation.4 | async-start | bytes 17039360 | tf_op jit(solution)/shard_map/all_gather | solution.py:142
  1064.1 21.1 %copy-start.7 = (bf16[8,512]{1,0:T(8,128)(2,1)S(1)}, bf16[8,512]{1,0:T(8,128)(2,1)}, u32[]{:S(2)}) copy-start(bf16[8,512]{1,0:T(8,128)(2,1)} %param.17) | copy-start | bytes 24580
  1064.1 22.7 %copy-start.10 = (s32[8]{0:T(128)S(1)}, s32[8]{0:T(128)}, u32[]{:S(2)}) copy-start(s32[8]{0:T(128)} %param.18) | copy-start | bytes 100
  1064.1 22.7 %copy-start.5 = (bf16[8,4096]{1,0:T(8,128)(2,1)S(1)}, bf16[8,4096]{1,0:T(8,128)(2,1)}, u32[]{:S(2)}) copy-start(bf16[8,4096]{1,0:T(8,128)(2,1)} %param.13) | copy-start | bytes 196612
  1064.1 22.7 %copy-start.9 = (bf16[8,512]{1,0:T(8,128)(2,1)S(1)}, bf16[8,512]{1,0:T(8,128)(2,1)}, u32[]{:S(2)}) copy-start(bf16[8,512]{1,0:T(8,128)(2,1)} %param.16) | copy-start | bytes 24580
  1064.1 22.9 %copy-start.3 = (bf16[8,64,512]{2,1,0:T(8,128)(2,1)S(1)}, bf16[8,64,512]{2,1,0:T(8,128)(2,1)}, u32[]{:S(2)}) copy-start(bf16[8,64,512]{2,1,0:T(8,128)(2,1)} %param.14) | copy-start | bytes 1572868
  1064.1 24.6 %copy-start.1 = (bf16[64,2048]{1,0:T(8,128)(2,1)S(1)}, bf16[64,2048]{1,0:T(8,128)(2,1)}, u32[]{:S(2)}) copy-start(bf16[64,2048]{1,0:T(8,128)(2,1)} %fusion.11) | copy-start | bytes 786436
  1064.2 24.6 %copy-start.4 = (bf16[2048,64]{0,1:T(8,128)(2,1)S(1)}, bf16[2048,64]{0,1:T(8,128)(2,1)}, u32[]{:S(2)}) copy-start(bf16[2048,64]{0,1:T(8,128)(2,1)} %param.21) | copy-start | bytes 786436
  1064.2 399.7 %all-to-all-start.3 = ((bf16[64,16,2048]{2,1,0:T(8,128)(2,1)}), bf16[64,16,2048]{2,1,0:T(8,128)(2,1)}, u32[]{:S(2)}, u32[]{:S(2)}) async-start(bf16[64,16,2048]{2,1,0:T(8,128)(2,1)} %bitcast.79), calls=%async_computation.3 | async-start | bytes 8388608 | tf_op jit(solution)/shard_map/all_to_all | solution.py:102
Sparse Core Ops, SparseCore 0:
  358.4 636.5 all-gather.2
where the time goes:
time: 1480 us
  blocking collectives  659 us (45%)
  waiting for transfers between devices  644 us (44%)
  starting transfers between devices  72.4 us (5%)
  local copies, waits for them, and re-layouts  45 us (3%)
  matrix products  29.1 us (2%)
    all_gather x1, blocking collectives, local(): lax.all_gather(expert_ids, EXPERT, axis=0, tiled=True)  652 us
    all_to_all x1, waiting for transfers between devices, expert_rows(): lax.all_to_all(expert_out.reshape(received.shape), EXPERT, split_axis=0,...  374 us
    all_to_all x1, waiting for transfers between devices, turned_blocks(): lax.all_to_all(tiles, axes[k], split_axis=k, concat_axis=k, tiled=True)  270 us
    all_to_all x1, starting transfers between devices, turned_blocks(): lax.all_to_all(tiles, axes[k], split_axis=k, concat_axis=k, tiled=True)  32.7 us
  transfers between devices with their start and end apart: 4, of which 2 were waited for; matrix products, arithmetic and copies ran while one was open for 3% of the time, Pallas kernels for 0%

commit v1 on v0

v1 whole, which is shorter than its diff:
```python
import functools
import math

import jax
import jax.numpy as jnp
from jax import lax
from jax.experimental import pallas as pl
from jax.experimental.pallas import tpu as pltpu
from jax.sharding import Mesh
from jax.sharding import PartitionSpec as P

HEADS = 32
KV_HEADS = 4
HEAD_DIM = 128
CTX = 64
EPSILON = 1e-06
SLOTS = 16
TEAM = 4
LANES = 128

MESH = pl.DeviceIdType.MESH
EXPERT = ("z", "core")
ALL = ("team", "quad", "z", "core")


def rms_normed(hidden_in, norm_gain):
    values = hidden_in.astype(jnp.float32)
    mean_square = jnp.mean(values * values, axis=-1, keepdims=True)
    return (values * lax.rsqrt(mean_square + EPSILON) * norm_gain.astype(jnp.float32)).astype(
        jnp.bfloat16
    )


def attend(queries, key_cache, value_cache, new_key, new_value, cache_lengths):
    seq_count = queries.shape[0]
    group_size = HEADS // KV_HEADS
    query_blocks = queries.reshape(seq_count, KV_HEADS, group_size, HEAD_DIM)
    cached_keys = key_cache.reshape(seq_count, CTX, KV_HEADS, HEAD_DIM)
    cached_values = value_cache.reshape(seq_count, CTX, KV_HEADS, HEAD_DIM)
    fresh_keys = new_key.reshape(seq_count, KV_HEADS, HEAD_DIM)
    fresh_values = new_value.astype(jnp.float32).reshape(seq_count, KV_HEADS, HEAD_DIM)
    score_scale = 1.0 / math.sqrt(HEAD_DIM)
    scores = (
        jnp.einsum("sgrd,scgd->sgrc", query_blocks, cached_keys, preferred_element_type=jnp.float32)
        * score_scale
    )
    own_score = (
        jnp.einsum("sgrd,sgd->sgr", query_blocks, fresh_keys, preferred_element_type=jnp.float32)
        * score_scale
    )
    positions = jnp.arange(CTX, dtype=jnp.int32)
    visible = positions[None, :] < cache_lengths[:, None]
    scores = jnp.where(visible[:, None, None, :], scores, -1e30)
    largest = jnp.maximum(jnp.max(scores, axis=-1), own_score)
    cached_exp = jnp.exp(scores - largest[..., None])
    own_exp = jnp.exp(own_score - largest)
    prob_total = jnp.sum(cached_exp, axis=-1) + own_exp
    cached_prob = (cached_exp / prob_total[..., None]).astype(jnp.bfloat16)
    own_prob = (own_exp / prob_total).astype(jnp.bfloat16).astype(jnp.float32)
    context = jnp.einsum(
        "sgrc,scgd->sgrd", cached_prob, cached_values, preferred_element_type=jnp.float32
    )
    context = context + own_prob[..., None] * fresh_values[:, :, None, :]
    return context.reshape(seq_count, HEADS * HEAD_DIM).astype(jnp.bfloat16)


def remote(src, dst, send, recv, to):
    return pltpu.make_async_remote_copy(
        src_ref=src, dst_ref=dst, send_sem=send, recv_sem=recv, device_id=to, device_id_type=MESH
    )


def wait_bytes(ref, sem):
    pltpu.make_async_copy(ref, ref, sem).wait()


def weights_kernel(nz, p_ref, out_ref, own_sem, send_sem, fwd_sem, recv_sem, mate_sem):
    quad, z, core = lax.axis_index("quad"), lax.axis_index("z"), lax.axis_index("core")
    me = z * 2 + core
    barrier = pltpu.get_barrier_semaphore()

    def greet(i, carry):
        for cc in range(2):
            pl.semaphore_signal(
                barrier, inc=1, device_id={"z": lax.rem(z + i, nz), "core": cc}, device_id_type=MESH
            )
        return carry

    lax.fori_loop(1, nz, greet, 0)
    pl.semaphore_signal(barrier, inc=1, device_id={"core": 1 - core}, device_id_type=MESH)
    for m in range(1, TEAM):
        pl.semaphore_signal(
            barrier, inc=1, device_id={"quad": lax.rem(quad + m, TEAM)}, device_id_type=MESH
        )
    pl.semaphore_wait(barrier, 2 * (nz - 1) + 1 + TEAM - 1)

    own = pltpu.make_async_copy(p_ref.at[me], out_ref.at[quad, me], own_sem)
    own.start()
    remote(
        p_ref.at[z * 2 + 1 - core], out_ref.at[quad, me], send_sem, recv_sem.at[0], {"core": 1 - core}
    ).start()

    def offset(i):
        k = i // 2 + 1
        return k + (i % 2) * (nz - 2 * k)

    def send(i, carry):
        ahead = offset(i)
        zz = lax.rem(z + ahead, nz)
        for cc in range(2):
            remote(
                p_ref.at[zz * 2 + cc],
                out_ref.at[quad, me],
                send_sem,
                recv_sem.at[ahead],
                {"z": zz, "core": cc},
            ).start()
        return carry

    lax.fori_loop(0, nz - 1, send, 0)

    def share(zz):
        rows = out_ref.at[quad, pl.ds(zz * 2, 2)]
        for m in range(1, TEAM):
            remote(
                rows, rows, fwd_sem, mate_sem.at[m - 1], {"quad": lax.rem(quad + m, TEAM)}
            ).start()

    own.wait()
    wait_bytes(out_ref.at[quad, z * 2 + 1 - core], recv_sem.at[0])
    share(z)

    def forward(i, carry):
        ahead = offset(i)
        zz = lax.rem(z - ahead + nz, nz)
        wait_bytes(out_ref.at[quad, pl.ds(zz * 2, 2)], recv_sem.at[ahead])
        share(zz)
        return carry

    lax.fori_loop(0, nz - 1, forward, 0)
    for m in range(1, TEAM):
        wait_bytes(out_ref.at[lax.rem(quad - m + TEAM, TEAM)], mate_sem.at[m - 1])
    wait_bytes(p_ref.at[pl.ds(0, 2 * nz - 1)], send_sem)
    wait_bytes(out_ref.at[pl.ds(0, TEAM - 1)], fwd_sem)


def move_weights(packed, nz):
    messages, rows, lanes = packed.shape
    return pl.pallas_call(
        functools.partial(weights_kernel, nz),
        name="move_weights",
        out_shape=jax.ShapeDtypeStruct((TEAM, messages, rows, lanes), packed.dtype),
        in_specs=[pl.BlockSpec(memory_space=pl.ANY)],
        out_specs=pl.BlockSpec(memory_space=pl.ANY),
        scratch_shapes=[
            pltpu.SemaphoreType.DMA,
            pltpu.SemaphoreType.DMA,
            pltpu.SemaphoreType.DMA,
            pltpu.SemaphoreType.DMA((nz,)),
            pltpu.SemaphoreType.DMA((TEAM - 1,)),
        ],
        compiler_params=pltpu.CompilerParams(collective_id=0, has_side_effects=True),
    )(packed)


def experts_kernel(
    nz,
    x_ref,
    meta_ref,
    w_ref,
    d_ref,
    o_ref,
    tokens,
    metas,
    wgu,
    mine,
    theirs,
    outgoing,
    acc,
    picked,
    hidden,
    sels,
    upper,
    local_sem,
    load_sem,
    ring_send,
    ring_meta_send,
    pair_send,
    pair_meta_send,
    out_send,
    sum_send,
    ring_recv,
    ring_meta,
    pair_recv,
    pair_meta,
    their_recv,
    sum_recv,
):
    half_ring = nz // 2
    z, core = lax.axis_index("z"), lax.axis_index("core")
    rows = x_ref.shape[0]
    half = rows // 2
    width = x_ref.shape[1]
    partner = {"core": 1 - core}
    after = {"z": lax.rem(z + 1, nz)}
    before = {"z": lax.rem(z + nz - 1, nz)}
    towards = (after, before)

    loads = [pltpu.make_async_copy(x_ref, tokens.at[z, 0], local_sem.at[0])]
    loads.append(pltpu.make_async_copy(meta_ref, metas.at[z, 0], local_sem.at[1]))
    for copy in loads:
        copy.start()
    strips = wgu.shape[2] // TEAM // LANES
    gate_rows = wgu.shape[1]
    weight_loads = []
    for quarter in range(TEAM):
        for strip in range(strips):
            weight_loads.append(
                pltpu.make_async_copy(
                    w_ref.at[quarter, :, pl.ds(strip * gate_rows, gate_rows), :],
                    wgu.at[:, :, pl.ds((quarter * strips + strip) * LANES, LANES)],
                    load_sem.at[quarter * strips + strip],
                )
            )
    for copy in weight_loads:
        copy.start()

    barrier = pltpu.get_barrier_semaphore()
    for who in (after, before, partner):
        pl.semaphore_signal(barrier, inc=1, device_id=who, device_id_type=MESH)
    pl.semaphore_wait(barrier, 3)
    for copy in loads:
        copy.wait()

    def chip_behind(way, s):
        return lax.rem(z + (nz - s if way == 0 else s), nz)

    def ring(way, s, part):
        at = tokens.at[chip_behind(way, s - 1), 0, pl.ds(part * half, half)]
        return remote(at, at, ring_send, ring_recv.at[way, s - 1, part], towards[way])

    def ring_metas(way, s):
        at = metas.at[chip_behind(way, s - 1), 0]
        return remote(at, at, ring_meta_send, ring_meta.at[way, s - 1], towards[way])

    def wait_ring(way, s, part):
        wait_bytes(
            tokens.at[chip_behind(way, s), 0, pl.ds(part * half, half)],
            ring_recv.at[way, s - 1, part],
        )

    def wait_ring_meta(way, s):
        wait_bytes(metas.at[chip_behind(way, s), 0], ring_meta.at[way, s - 1])

    def pair_up(t, way, s):
        remote(
            tokens.at[t, 0], tokens.at[t, 1], pair_send, pair_recv.at[way, s - 1], partner
        ).start()
        remote(
            metas.at[t, 0], metas.at[t, 1], pair_meta_send, pair_meta.at[way, s - 1], partner
        ).start()

    def wait_pair(t, way, s):
        wait_bytes(tokens.at[t, 1], pair_recv.at[way, s - 1])
        wait_bytes(metas.at[t, 1], pair_meta.at[way, s - 1])

    for way in range(2):
        ring_metas(way, 1).start()
        for part in range(2):
            ring(way, 1, part).start()
    pair_up(z, 1, half_ring)

    across = lax.broadcasted_iota(jnp.int32, (LANES, LANES), 1)
    down = lax.broadcasted_iota(jnp.int32, (LANES, LANES), 0)
    upper[...] = jnp.where(
        (down < across) & ((down >= rows) == (across >= rows)), 1.0, 0.0
    ).astype(jnp.bfloat16)
    for copy in weight_loads:
        copy.wait()

    expert = (z * 2 + core).astype(jnp.float32)

    def routing(t):
        own, other = metas[t, 0], metas[t, 1]
        lane = lax.broadcasted_iota(jnp.int32, own.shape, 1)
        ids = jnp.where(lane < rows, own, pltpu.roll(other, rows, 1))
        weights = jnp.where(lane < rows, pltpu.roll(own, rows, 1), other)
        same = ids == expert
        hit = jnp.sum(jnp.where(same, 1.0, 0.0), axis=0, keepdims=True)
        mix = jnp.sum(jnp.where(same, weights, 0.0), axis=0, keepdims=True)
        hits = jnp.broadcast_to(hit, own.shape).astype(jnp.bfloat16)
        rank = jnp.dot(hits, upper[...], preferred_element_type=jnp.float32)[0:1]
        lane = lax.broadcasted_iota(jnp.int32, (2 * SLOTS, LANES), 1)
        slot = lax.broadcasted_iota(jnp.int32, (2 * SLOTS, LANES), 0)
        rank = rank + jnp.where(lane < rows, 0.0, float(SLOTS))
        sel = jnp.where((slot.astype(jnp.float32) == rank) & (hit > 0.5), 1.0, 0.0)
        return sel, jnp.sum(sel * mix, axis=1, keepdims=True)

    def chips(s):
        return (lax.rem(z - s + nz, nz), lax.rem(z + lax.rem(s, half_ring), nz))

    def first_part(s):
        mixes = []
        for i, t in enumerate(chips(s)):
            sel, mix = routing(t)
            sels[i] = sel
            mixes.append(mix)
            picked[pl.ds(2 * SLOTS * i, 2 * SLOTS), :] = jnp.dot(
                sel.astype(jnp.bfloat16),
                tokens[t].reshape(2 * rows, width),
                preferred_element_type=jnp.float32,
            ).astype(jnp.bfloat16)
        mix = jnp.concatenate(mixes, axis=0)
        gate_up = jnp.dot(
            picked[...], wgu[...].reshape(width, -1), preferred_element_type=jnp.float32
        )
        ff = gate_up.shape[1] // 2
        gate, up = gate_up[:, :ff], gate_up[:, ff:]
        hidden[...] = (gate / (1.0 + jnp.exp(-gate)) * up * mix).astype(jnp.bfloat16)

    def second_part(s):
        spot = lax.rem(s, 2)

        @pl.when(s > 2)
        def _():
            wait_bytes(outgoing.at[spot], out_send.at[spot])

        rows_out = jnp.dot(hidden[...], d_ref[...], preferred_element_type=jnp.float32).astype(
            jnp.bfloat16
        )
        for i, t in enumerate(chips(s)):
            spread = lax.dot_general(
                sels[i].astype(jnp.bfloat16),
                rows_out[2 * SLOTS * i : 2 * SLOTS * (i + 1)],
                (((0,), (0,)), ((), ())),
                preferred_element_type=jnp.float32,
            ).astype(jnp.bfloat16)
            mine[t] = spread[:rows]
            outgoing[spot, i] = spread[rows:]
        for i, t in enumerate(chips(s)):
            remote(
                outgoing.at[spot, i],
                theirs.at[t],
                out_send.at[spot],
                their_recv.at[i, s - 1],
                partner,
            ).start()

    def wait_chunk(s):
        wait_pair(chip_behind(0, s), 0, s)
        wait_pair(chip_behind(1, s), 1, s)

    def step(s, carry):
        for way in range(2):
            wait_ring_meta(way, s)
            ring_metas(way, s + 1).start()
            wait_ring(way, s, 0)
            ring(way, s + 1, 0).start()

        @pl.when(s > 1)
        def _():
            wait_chunk(s - 1)
            first_part(s - 1)

        for way in range(2):
            wait_ring(way, s, 1)
            ring(way, s + 1, 1).start()
            pair_up(chip_behind(way, s), way, s)

        @pl.when(s > 1)
        def _():
            second_part(s - 1)

        return carry

    lax.fori_loop(1, half_ring - 1, step, 0)

    s = half_ring - 1
    for way in range(2):
        wait_ring_meta(way, s)
        if way == 0:
            ring_metas(way, s + 1).start()
        wait_ring(way, s, way)
        ring(way, s + 1, way).start()
        wait_ring(way, s, 1 - way)
        pair_up(chip_behind(way, s), way, s)
    wait_chunk(s - 1)
    first_part(s - 1)
    second_part(s - 1)

    s = half_ring
    wait_ring_meta(0, s)
    wait_ring(0, s, 0)
    wait_ring(1, s, 1)
    far = chip_behind(0, s)
    pair_up(far, 0, s)
    wait_chunk(s - 1)
    first_part(s - 1)
    second_part(s - 1)
    wait_pair(far, 0, s)
    wait_pair(z, 1, s)
    first_part(s)
    second_part(s)

    def block(way, d):
        return lax.rem(z + (d if way == 0 else nz - d), nz)

    def wait_their(i, s):
        wait_bytes(theirs.at[chips(s)[i]], their_recv.at[i, s - 1])

    def onward(way, j, part):
        return remote(
            acc.at[way, j, pl.ds(part * half, half)],
            acc.at[way, j + 1, pl.ds(part * half, half)],
            sum_send,
            sum_recv.at[way, j, part],
            towards[way],
        )

    def add(way, j, t, part, fresh):
        at = pl.ds(part * half, half)
        total = mine[t, at, :].astype(jnp.float32) + theirs[t, at, :].astype(jnp.float32)
        if not fresh:
            total = total + acc[way, j, at, :].astype(jnp.float32)
        acc[way, j, at, :] = total.astype(jnp.bfloat16)

    def wait_sum(way, j, part):
        wait_bytes(acc.at[way, j, pl.ds(part * half, half)], sum_recv.at[way, j - 1, part])

    wait_their(0, half_ring)
    for way in range(2):
        add(way, 0, far, way, True)
    for way in range(2):
        onward(way, 0, way).start()

    d = half_ring - 1
    wait_their(0, d)
    wait_their(1, d)
    for way in range(2):
        add(way, 1, block(way, d), 1 - way, True)
    for way in range(2):
        onward(way, 1, 1 - way).start()
    for way in range(2):
        wait_sum(way, 1, way)
        add(way, 1, block(way, d), way, False)
    for way in range(2):
        onward(way, 1, way).start()

    def sums(j, carry):
        d = half_ring - j
        wait_their(0, d)
        wait_their(1, d)
        for part in range(2):
            for way in range(2):
                wait_sum(way, j, part)
                add(way, j, block(way, d), part, False)
            for way in range(2):
                onward(way, j, part).start()
        return carry

    lax.fori_loop(2, half_ring, sums, 0)

    wait_their(1, half_ring)
    for part in range(2):
        at = pl.ds(part * half, half)
        for way in range(2):
            wait_sum(way, half_ring, part)
        o_ref[at, :] = (
            mine[z, at, :].astype(jnp.float32)
            + theirs[z, at, :].astype(jnp.float32)
            + acc[0, half_ring, at, :].astype(jnp.float32)
            + acc[1, half_ring, at, :].astype(jnp.float32)
        ).astype(jnp.bfloat16)

    wait_bytes(mine.at[pl.ds(0, nz - 1)], ring_send)
    wait_bytes(metas.at[pl.ds(0, nz - 1), 0], ring_meta_send)
    wait_bytes(mine, pair_send)
    wait_bytes(metas.at[:, 0], pair_meta_send)
    wait_bytes(mine.at[pl.ds(0, nz - 1)], sum_send)
    wait_bytes(outgoing.at[0], out_send.at[0])
    wait_bytes(outgoing.at[1], out_send.at[1])


def experts(normed, meta, moved, down, nz):
    rows, width = normed.shape
    ff = down.shape[0]
    bf16 = jnp.bfloat16
    steps = nz // 2
    dma = pltpu.SemaphoreType.DMA
    return pl.pallas_call(
        functools.partial(experts_kernel, nz),
        name="experts",
        out_shape=jax.ShapeDtypeStruct((rows, width), bf16),
        in_specs=[
            pl.BlockSpec(memory_space=pl.ANY),
            pl.BlockSpec(memory_space=pl.ANY),
            pl.BlockSpec(memory_space=pl.ANY),
            pl.BlockSpec(memory_space=pltpu.VMEM),
        ],
        out_specs=pl.BlockSpec(memory_space=pltpu.VMEM),
        scratch_shapes=[
            pltpu.VMEM((nz, 2, rows, width), bf16),
            pltpu.VMEM((nz, 2, 8, LANES), jnp.float32),
            pltpu.VMEM((2 * nz, width // (2 * nz), 2 * ff), bf16),
            pltpu.VMEM((nz, rows, width), bf16),
            pltpu.VMEM((nz, rows, width), bf16),
            pltpu.VMEM((2, 2, rows, width), bf16),
            pltpu.VMEM((2, steps + 1, rows, width), bf16),
            pltpu.VMEM((4 * SLOTS, width), bf16),
            pltpu.VMEM((4 * SLOTS, ff), bf16),
            pltpu.VMEM((2, 2 * SLOTS, LANES), jnp.float32),
            pltpu.VMEM((LANES, LANES), bf16),
            dma((2,)),
            dma((3 * TEAM,)),
            dma,
            dma,
            dma,
            dma,
            dma((2,)),
            dma,
            dma((2, steps, 2)),
            dma((2, steps)),
            dma((2, steps)),
            dma((2, steps)),
            dma((2, steps)),
            dma((2, steps, 2)),
        ],
        compiler_params=pltpu.CompilerParams(
            collective_id=1, has_side_effects=True, vmem_limit_bytes=60 << 20
        ),
    )(normed, meta, moved, down)


def pack(gate, up, down, quad):
    count, gate_rows, ff = gate.shape
    down_rows, width = down.shape[1:]
    cut, down_cut = 2 * ff // TEAM, width // TEAM
    start = lax.rem(quad, TEAM // 2) * cut
    gate_up = jnp.where(
        quad < TEAM // 2,
        lax.dynamic_slice_in_dim(gate, start, cut, 2),
        lax.dynamic_slice_in_dim(up, start, cut, 2),
    )
    down = lax.dynamic_slice_in_dim(down, quad * down_cut, down_cut, 2)
    strips = [
        jnp.swapaxes(a.reshape(count, a.shape[1], -1, LANES), 1, 2).reshape(count, -1, LANES)
        for a in (gate_up, down)
    ]
    return jnp.concatenate(strips, axis=1)


def local(
    nz,
    queries,
    key_cache,
    value_cache,
    new_key,
    new_value,
    cache_lengths,
    hidden_in,
    norm_gain,
    router_weight,
    expert_ids,
    gate_train,
    up_train,
    down_train,
):
    quad = lax.axis_index("quad")
    moved = move_weights(pack(gate_train, up_train, down_train, quad), nz)
    attended = attend(queries, key_cache, value_cache, new_key, new_value, cache_lengths)

    normed = rms_normed(hidden_in, norm_gain)
    logits = jnp.dot(normed, router_weight, preferred_element_type=jnp.float32)
    expert_range = jnp.arange(router_weight.shape[1], dtype=jnp.int32)
    picked = expert_ids[:, :, None] == expert_range[None, None, :]
    chosen = jnp.sum(jnp.where(picked, logits[:, None, :], 0.0), axis=-1)
    mixing = jax.nn.softmax(chosen, axis=-1)
    meta = jnp.concatenate([expert_ids.astype(jnp.float32).T, mixing.T], axis=1)

    gate_rows, down_rows = gate_train.shape[1], down_train.shape[1]
    strips = 2 * gate_train.shape[2] // TEAM // LANES
    down = moved[:, :, strips * gate_rows :, :].reshape(TEAM, 2 * nz, -1, down_rows, LANES)
    down = jnp.transpose(down, (1, 3, 0, 2, 4)).reshape(2 * nz * down_rows, -1)
    return attended, experts(normed, meta, moved, down, nz)


def solution(mesh):
    groups, nz = mesh.shape["groups"], mesh.shape["expert"] // 2
    torus = Mesh(mesh.devices.reshape(groups // TEAM, TEAM, nz, 2), ALL)
    placed = (
        P(ALL, None),
        P(ALL, None, None),
        P(ALL, None, None),
        P(ALL, None),
        P(ALL, None),
        P(ALL),
        P(ALL, None),
        P(),
        P(),
        P(ALL, None),
        P(None, EXPERT, None),
        P(None, EXPERT, None),
        P(None, EXPERT, None),
    )
    return jax.shard_map(
        functools.partial(local, nz),
        mesh=torus,
        in_specs=placed,
        out_specs=(P(ALL, None), P(ALL, None)),
        check_vma=False,
    )
```

time: 1480 us -> 496 us (0.34)
  blocking collectives: 659 us -> 0 us
  waiting for transfers between devices: 644 us -> 0 us
  Pallas kernels: 0 us -> 454 us
  starting transfers between devices: 72.4 us -> 0 us
  matrix products: 29.1 us -> 3.25 us
  local copies, waits for them, and re-layouts: 45 us -> 29.1 us
    all_gather x1 -> x0, blocking collectives: 652 us -> none  [local(): lax.all_gather(expert_ids, EXPERT, axis=0, tiled=True)]
    all_to_all x3 -> x0, waiting for transfers between devices: 644 us -> none  [the longest x1 374 us: expert_rows(): lax.all_to_all(expert_out.reshape(received.shape), EXPERT, split_axis=0,...]
    pallas_call x0 -> x2, Pallas kernels: none -> 454 us  [the longest x1 228 us: move_weights(): pl.pallas_call(functools.partial(weights_kernel, nz), name='move_weights'...]
    all_to_all x3 -> x0, starting transfers between devices: 72.3 us -> none  [the longest x1 32.7 us: turned_blocks(): lax.all_to_all(tiles, axes[k], split_axis=k, concat_axis=k, tiled=True)]
    dot_general x3 -> x0, matrix products: 27.9 us -> none  [the longest x1 13.7 us: expert_rows(): jnp.dot(hidden_units, down_weight, preferred_element_type=jnp.float32)]
    gather x1 -> x0, local copies, waits for them, and re-layouts: 16.7 us -> none  [local(): jnp.take(all_rows, row_index.reshape(-1), axis=0)]
    another operation x7 -> x0, local copies, waits for them, and re-layouts: 15.8 us -> none  [the longest x2 9.32 us: turned_blocks(): tiles = tiles.reshape(*dims, *tiles.shape[1:])]
  transfers between devices with their start and end apart: 4 -> 0, of which waited for: 2 -> 0; matrix products, arithmetic and copies ran while one was open for 3% -> 0% of each run, Pallas kernels for 0% -> 0%
where the time goes in v1:
time: 496 us; the launch traced here: 495 us
  Pallas kernels  454 us (92%)
  local copies, waits for them, and re-layouts  29.1 us (6%)
  other arithmetic  7.78 us (2%)
    pallas_call x1, Pallas kernels, move_weights(): pl.pallas_call(functools.partial(weights_kernel, nz), name='move_weights'...  228 us
    pallas_call x1, Pallas kernels, experts(): pl.pallas_call(functools.partial(experts_kernel, nz), name='experts', out...  226 us

profile of v1, /device:TPU:38, one launch (start us, length us, event | category | flops | bytes accessed | tf_op | source)
XLA Modules:
  0.0 495.2 jit_solution(2984279474019063642)
XLA Ops:
  0.6 0.0 copy-start
  0.7 3.6 dynamic-slice_select_fusion
  4.3 5.1 %reshape.74 = bf16[64,32,3,128]{3,2,1,0:T(4,128)(2,1)} reshape(bf16[64,32,384]{2,1,0:T(8,128)(2,1)} %dynamic-slice_select_fusion) | data formatting | bytes 3145728 | tf_op jit(solution)/shard_map/reshape | solution.py:546
  9.4 3.1 copy.38
  12.5 0.0 copy-done
  12.5 1.0 constant_dynamic-slice_fusion
  13.4 2.5 reshape.76
  15.9 0.0 copy-start.1
  15.9 1.4 copy.39
  17.3 0.5 copy.40
  17.8 0.0 copy-done.1
  17.8 1.6 pad_maximum_fusion.p_ref
  19.4 227.9 %move_weights.1.w_ref = bf16[4,64,144,128]{3,2,1,0:T(8,128)(2,1)} custom-call(bf16[64,144,128]{2,1,0:T(8,128)(2,1)} %pad_maximum_fusion.p_ref), custom_call_target="tpu_custom_call" | custom-call | tf_op jit(solution)/shard_map/move_weights/pallas_call | solution.py:149
  247.3 0.0 slice-start
  247.3 1.9 slice-done
  249.2 0.8 copy.41
  250.1 4.1 copy.42
  254.2 0.0 copy-start.8
  254.2 0.0 copy-start.3
  254.2 6.2 %reshape.79.d_ref = bf16[768,2048]{1,0:T(8,128)(2,1)} reshape(bf16[64,12,4,4,128]{4,3,2,1,0:T(4,128)(2,1)} %copy.42) | data formatting | bytes 6291456 | tf_op jit(solution)/shard_map/reshape | solution.py:583
  260.3 0.0 copy-done.8
  260.3 0.0 copy-done.3
  260.4 0.2 fusion.3
  260.5 1.1 fusion.5.x_ref
  261.6 0.0 copy-start.2
  261.6 1.3 fusion.21
  262.9 0.0 copy-done.6
  262.9 0.1 copy.36
  263.0 0.2 select_reduce_fusion
  263.2 0.1 copy.37
  263.3 0.1 reduce_max.19
  263.4 0.7 pad_maximum_fusion.1.meta_ref
  264.1 0.0 copy-done.2
  264.1 0.0 copy-start.9
  264.1 0.0 copy-start.7
  264.1 226.3 %experts.1 = bf16[64,2048]{1,0:T(8,128)(2,1)} custom-call(bf16[64,2048]{1,0:T(8,128)(2,1)} %copy-done.2, f32[8,128]{1,0:T(8,128)} %pad_maximum_fusion.1.meta_ref, bf16[4,64,144,128]{3,2,1,0:T(8,128)(2,1)} %move_weights.1.w_ref, bf16[768,2048]{1,0:T(8,128)(2,1)} %reshape.79.d_ref), custom_call_target="tpu_custom_call" | custom-call | tf_op jit(solution)/shard_map/experts/pallas_call | solution.py:490
  490.5 0.0 copy-done.10
  490.5 0.1 iota_compare_fusion.1
  490.6 0.0 copy-done.4
  490.6 0.0 copy-done.5
  490.6 0.5 fusion.20
  491.0 0.0 copy-done.9
  491.0 0.2 fusion.13
  491.2 0.2 fusion.10
  491.5 0.0 copy-done.7
  491.5 1.4 fusion.2
  492.9 0.7 copy.67
  493.5 1.7 copy.69
  (13 shorter events, 0.1 us)
Async XLA Ops:
  0.6 11.8 %copy-start = (bf16[64,12,2048]{2,0,1:T(8,128)(2,1)S(1)}, bf16[64,12,2048]{2,0,1:T(8,128)(2,1)}, u32[]{:S(2)}) copy-start(bf16[64,12,2048]{2,0,1:T(8,128)(2,1)} %param.25) | copy-start | bytes 9437188
  15.9 2.0 copy-start.1
  247.3 1.9 slice-start
  254.2 6.2 %copy-start.8 = (bf16[2048]{0:T(1024)(128)(2,1)S(1)}, bf16[2048]{0:T(1024)(128)(2,1)}, u32[]{:S(2)}) copy-start(bf16[2048]{0:T(1024)(128)(2,1)} %param.20) | copy-start | bytes 12292
  254.2 6.2 %copy-start.3 = (bf16[64,2048]{1,0:T(8,128)(2,1)S(1)}, bf16[64,2048]{1,0:T(8,128)(2,1)}, u32[]{:S(2)}) copy-start(bf16[64,2048]{1,0:T(8,128)(2,1)} %param.19) | copy-start | bytes 786436
  254.2 8.7 %copy-start.6 = (s32[64,8]{0,1:T(8,128)S(1)}, s32[64,8]{0,1:T(8,128)}, u32[]{:S(2)}) copy-start(s32[64,8]{0,1:T(8,128)} %param.22) | copy-start | bytes 6148
  261.6 2.5 copy-start.2
  264.1 226.4 %copy-start.10 = (s32[8]{0:T(128)S(1)}, s32[8]{0:T(128)}, u32[]{:S(2)}) copy-start(s32[8]{0:T(128)} %param.18) | copy-start | bytes 100
  264.1 226.4 %copy-start.4 = (bf16[8,64,512]{2,1,0:T(8,128)(2,1)S(1)}, bf16[8,64,512]{2,1,0:T(8,128)(2,1)}, u32[]{:S(2)}) copy-start(bf16[8,64,512]{2,1,0:T(8,128)(2,1)} %param.14) | copy-start | bytes 1572868
  264.1 226.4 %copy-start.5 = (bf16[8,4096]{1,0:T(8,128)(2,1)S(1)}, bf16[8,4096]{1,0:T(8,128)(2,1)}, u32[]{:S(2)}) copy-start(bf16[8,4096]{1,0:T(8,128)(2,1)} %param.13) | copy-start | bytes 196612
  264.1 226.9 %copy-start.9 = (bf16[8,512]{1,0:T(8,128)(2,1)S(1)}, bf16[8,512]{1,0:T(8,128)(2,1)}, u32[]{:S(2)}) copy-start(bf16[8,512]{1,0:T(8,128)(2,1)} %param.16) | copy-start | bytes 24580
  264.1 227.3 %copy-start.7 = (bf16[8,512]{1,0:T(8,128)(2,1)S(1)}, bf16[8,512]{1,0:T(8,128)(2,1)}, u32[]{:S(2)}) copy-start(bf16[8,512]{1,0:T(8,128)(2,1)} %param.17) | copy-start | bytes 24580

commit v2 on v1

--- a/solution.py
+++ b/solution.py
@@ -74,50 +74,50 @@
     pltpu.make_async_copy(ref, ref, sem).wait()
 
 
-def weights_kernel(nz, p_ref, out_ref, own_sem, send_sem, fwd_sem, recv_sem, mate_sem):
+def weights_kernel(
+    nz, p_ref, out_ref, transit, own_sem, pair_send, ring_send, fwd_sem, recv_sem, hop_recv, mate_sem
+):
     quad, z, core = lax.axis_index("quad"), lax.axis_index("z"), lax.axis_index("core")
+    half_ring = nz // 2
     me = z * 2 + core
+    partner = {"core": 1 - core}
+
+    def chip(way, steps):
+        return lax.rem(z + (steps if way == 0 else nz - steps), nz)
+
+    next_chip = (chip(0, 1), chip(1, 1))
     barrier = pltpu.get_barrier_semaphore()
-
-    def greet(i, carry):
-        for cc in range(2):
-            pl.semaphore_signal(
-                barrier, inc=1, device_id={"z": lax.rem(z + i, nz), "core": cc}, device_id_type=MESH
-            )
-        return carry
-
-    lax.fori_loop(1, nz, greet, 0)
-    pl.semaphore_signal(barrier, inc=1, device_id={"core": 1 - core}, device_id_type=MESH)
-    for m in range(1, TEAM):
-        pl.semaphore_signal(
-            barrier, inc=1, device_id={"quad": lax.rem(quad + m, TEAM)}, device_id_type=MESH
-        )
-    pl.semaphore_wait(barrier, 2 * (nz - 1) + 1 + TEAM - 1)
+    friends = [{"z": next_chip[way], "core": cc} for way in range(2) for cc in range(2)]
+    friends += [partner] + [{"quad": lax.rem(quad + m, TEAM)} for m in range(1, TEAM)]
+    for who in friends:
+        pl.semaphore_signal(barrier, inc=1, device_id=who, device_id_type=MESH)
+    pl.semaphore_wait(barrier, len(friends))
 
     own = pltpu.make_async_copy(p_ref.at[me], out_ref.at[quad, me], own_sem)
     own.start()
-    remote(
-        p_ref.at[z * 2 + 1 - core], out_ref.at[quad, me], send_sem, recv_sem.at[0], {"core": 1 - core}
-    ).start()
-
-    def offset(i):
-        k = i // 2 + 1
-        return k + (i % 2) * (nz - 2 * k)
-
-    def send(i, carry):
-        ahead = offset(i)
-        zz = lax.rem(z + ahead, nz)
-        for cc in range(2):
-            remote(
-                p_ref.at[zz * 2 + cc],
-                out_ref.at[quad, me],
-                send_sem,
-                recv_sem.at[ahead],
-                {"z": zz, "core": cc},
-            ).start()
-        return carry
-
-    lax.fori_loop(0, nz - 1, send, 0)
+
+    def place(hops, dist):
+        return half_ring * (hops - 1) - hops * (hops - 1) // 2 + half_ring - dist
+
+    def pair_at(hops, way, dist):
+        return transit.at[way, place(hops, dist)]
+
+    def single_at(hops, way):
+        return transit.at[way, place(hops, half_ring), pl.ds(0, 1)]
+
+    def pass_on(way, src, dst, hops, dist):
+        remote(
+            src, dst, ring_send.at[way], hop_recv.at[way, place(hops, dist)], {"z": next_chip[way]}
+        ).start()
+
+    def deliver(way, src, hops, dist, cc):
+        remote(
+            src,
+            out_ref.at[quad, chip(way, nz - hops) * 2 + core],
+            ring_send.at[way],
+            recv_sem.at[dist if way == 0 else nz - dist],
+            {"z": next_chip[way], "core": cc},
+        ).start()
 
     def share(zz):
         rows = out_ref.at[quad, pl.ds(zz * 2, 2)]
@@ -126,41 +126,99 @@
                 rows, rows, fwd_sem, mate_sem.at[m - 1], {"quad": lax.rem(quad + m, TEAM)}
             ).start()
 
+    def arrived(ahead):
+        zz = lax.rem(z - ahead + nz, nz)
+        wait_bytes(out_ref.at[quad, pl.ds(zz * 2, 2)], recv_sem.at[ahead])
+        share(zz)
+
+    for way in range(2):
+        at = pl.ds(chip(way, half_ring) * 2 + way, 1)
+        pass_on(way, p_ref.at[at], single_at(1, way), 1, half_ring)
+
+    def first(i, carry):
+        dist = half_ring - 1 - i
+        for way in range(2):
+            at = pl.ds(chip(way, dist) * 2, 2)
+            pass_on(way, p_ref.at[at], pair_at(1, way, dist), 1, dist)
+        return carry
+
+    lax.fori_loop(0, half_ring - 2, first, 0)
+    for way in range(2):
+        for cc in range(2):
+            deliver(way, p_ref.at[chip(way, 1) * 2 + cc], 0, 1, cc)
+    remote(
+        p_ref.at[z * 2 + 1 - core], out_ref.at[quad, me], pair_send, recv_sem.at[0], partner
+    ).start()
     own.wait()
     wait_bytes(out_ref.at[quad, z * 2 + 1 - core], recv_sem.at[0])
     share(z)
 
-    def forward(i, carry):
-        ahead = offset(i)
-        zz = lax.rem(z - ahead + nz, nz)
-        wait_bytes(out_ref.at[quad, pl.ds(zz * 2, 2)], recv_sem.at[ahead])
-        share(zz)
+    def relay(hops, carry):
+        for way in range(2):
+            src = single_at(hops, way)
+            wait_bytes(src, hop_recv.at[way, place(hops, half_ring)])
+            pass_on(way, src, single_at(hops + 1, way), hops + 1, half_ring)
+
+        def through(i, carry):
+            dist = half_ring - 1 - i
+            for way in range(2):
+                src = pair_at(hops, way, dist)
+                wait_bytes(src, hop_recv.at[way, place(hops, dist)])
+                pass_on(way, src, pair_at(hops + 1, way, dist), hops + 1, dist)
+            return carry
+
+        lax.fori_loop(0, half_ring - 2 - hops, through, 0)
+        for way in range(2):
+            src = pair_at(hops, way, hops + 1)
+            wait_bytes(src, hop_recv.at[way, place(hops, hops + 1)])
+            for cc in range(2):
+                deliver(way, src.at[cc], hops, hops + 1, cc)
+        arrived(hops)
+        arrived(nz - hops)
         return carry
 
-    lax.fori_loop(0, nz - 1, forward, 0)
+    lax.fori_loop(1, half_ring - 1, relay, 0)
+    hops = half_ring - 1
+    for way in range(2):
+        src = single_at(hops, way)
+        wait_bytes(src, hop_recv.at[way, place(hops, half_ring)])
+        deliver(way, src.at[0], hops, half_ring, way)
+    arrived(hops)
+    arrived(nz - hops)
+    arrived(half_ring)
     for m in range(1, TEAM):
         wait_bytes(out_ref.at[lax.rem(quad - m + TEAM, TEAM)], mate_sem.at[m - 1])
-    wait_bytes(p_ref.at[pl.ds(0, 2 * nz - 1)], send_sem)
+    wait_bytes(p_ref.at[0], pair_send)
+    for way in range(2):
+        wait_bytes(out_ref.at[pl.ds(0, nz // 8)], ring_send.at[way])
     wait_bytes(out_ref.at[pl.ds(0, TEAM - 1)], fwd_sem)
 
 
 def move_weights(packed, nz):
     messages, rows, lanes = packed.shape
+    half_ring = nz // 2
+    places = half_ring * (half_ring - 1) // 2
+    dma = pltpu.SemaphoreType.DMA
     return pl.pallas_call(
         functools.partial(weights_kernel, nz),
         name="move_weights",
-        out_shape=jax.ShapeDtypeStruct((TEAM, messages, rows, lanes), packed.dtype),
+        out_shape=(
+            jax.ShapeDtypeStruct((TEAM, messages, rows, lanes), packed.dtype),
+            jax.ShapeDtypeStruct((2, places, 2, rows, lanes), packed.dtype),
+        ),
         in_specs=[pl.BlockSpec(memory_space=pl.ANY)],
-        out_specs=pl.BlockSpec(memory_space=pl.ANY),
+        out_specs=[pl.BlockSpec(memory_space=pl.ANY)] * 2,
         scratch_shapes=[
-            pltpu.SemaphoreType.DMA,
-            pltpu.SemaphoreType.DMA,
-            pltpu.SemaphoreType.DMA,
-            pltpu.SemaphoreType.DMA((nz,)),
-            pltpu.SemaphoreType.DMA((TEAM - 1,)),
+            dma,
+            dma,
+            dma((2,)),
+            dma,
+            dma((nz,)),
+            dma((2, places)),
+            dma((TEAM - 1,)),
         ],
         compiler_params=pltpu.CompilerParams(collective_id=0, has_side_effects=True),
-    )(packed)
+    )(packed)[0]
 
 
 def experts_kernel(

time: 496 us -> 492 us (level)
    pallas_call x1, Pallas kernels: 226 us -> 200 us  [experts(): pl.pallas_call(functools.partial(experts_kernel, nz), name='experts', out...]
    pallas_call x1, Pallas kernels: 228 us -> 250 us  [move_weights(): pl.pallas_call(functools.partial(weights_kernel, nz), name='move_weights'...]
where the time goes in v2:
time: 492 us; the launch traced here: 491 us
  Pallas kernels  450 us (91%)
  local copies, waits for them, and re-layouts  29.7 us (6%)
  other arithmetic  7.79 us (2%)
    pallas_call x1, Pallas kernels, move_weights(): pl.pallas_call(functools.partial(weights_kernel, nz), name='move_weights'...  250 us
    pallas_call x1, Pallas kernels, experts(): pl.pallas_call(functools.partial(experts_kernel, nz), name='experts', out...  200 us

profile of v2, /device:TPU:38, one launch (start us, length us, event | category | flops | bytes accessed | tf_op | source)
XLA Modules:
  0.0 491.5 jit_solution(13825643731625074984)
XLA Ops:
  0.6 0.0 copy-start
  0.7 3.6 dynamic-slice_select_fusion
  4.3 5.1 %reshape.74 = bf16[64,32,3,128]{3,2,1,0:T(4,128)(2,1)} reshape(bf16[64,32,384]{2,1,0:T(8,128)(2,1)} %dynamic-slice_select_fusion) | data formatting | bytes 3145728 | tf_op jit(solution)/shard_map/reshape | solution.py:604
  9.4 3.1 copy.38
  12.5 0.0 copy-done
  12.5 1.0 constant_dynamic-slice_fusion
  13.4 2.5 reshape.76
  15.9 0.0 copy-start.1
  15.9 1.4 copy.39
  17.3 0.5 copy.40
  17.8 0.0 copy-done.1
  17.9 1.6 pad_maximum_fusion.p_ref
  19.4 250.0 %move_weights.1 = (bf16[4,64,144,128]{3,2,1,0:T(8,128)(2,1)}, bf16[2,120,2,144,128]{4,3,2,1,0:T(8,128)(2,1)}) custom-call(bf16[64,144,128]{2,1,0:T(8,128)(2,1)} %pad_maximum_fusion.p_ref), custom_call_target="tpu_custom_call" | custom-call | tf_op jit(solution)/shard_map/move_weights/pallas_call | solution.py:202
  269.5 2.5 slice.3
  271.9 0.8 copy.41
  272.8 4.1 copy.42
  276.9 0.0 copy-start.8
  276.9 0.0 copy-start.3
  276.9 0.0 copy-start.6
  276.9 6.2 %reshape.79.d_ref = bf16[768,2048]{1,0:T(8,128)(2,1)} reshape(bf16[64,12,4,4,128]{4,3,2,1,0:T(4,128)(2,1)} %copy.42) | data formatting | bytes 6291456 | tf_op jit(solution)/shard_map/reshape | solution.py:641
  283.1 0.0 copy-done.8
  283.1 0.0 copy-done.3
  283.1 0.2 fusion.3
  283.2 1.1 fusion.5.x_ref
  284.3 0.0 copy-start.2
  284.3 1.3 fusion.21
  285.6 0.0 copy-done.6
  285.6 0.1 copy.36
  285.7 0.2 select_reduce_fusion
  285.9 0.1 copy.37
  286.0 0.1 reduce_max.19
  286.2 0.7 pad_maximum_fusion.1.meta_ref
  286.8 0.0 copy-done.2
  286.8 0.0 copy-start.9
  286.9 0.0 copy-start.7
  286.9 199.8 %experts.1 = bf16[64,2048]{1,0:T(8,128)(2,1)} custom-call(bf16[64,2048]{1,0:T(8,128)(2,1)} %copy-done.2, f32[8,128]{1,0:T(8,128)} %pad_maximum_fusion.1.meta_ref, bf16[4,64,144,128]{3,2,1,0:T(8,128)(2,1)} %get-tuple-element.3.w_ref, bf16[768,2048]{1,0:T(8,128)(2,1)} %reshape.79.d_ref), custom_call_target="tpu_custom_call" | custom-call | tf_op jit(solution)/shard_map/experts/pallas_call | solution.py:548
  486.7 0.0 copy-done.10
  486.7 0.1 iota_compare_fusion.1
  486.8 0.0 copy-done.4
  486.8 0.0 copy-done.5
  486.8 0.5 fusion.20
  487.3 0.0 copy-done.9
  487.3 0.2 fusion.13
  487.5 0.2 fusion.10
  487.7 0.0 copy-done.7
  487.8 1.4 fusion.2
  489.1 0.7 copy.67
  489.8 1.7 copy.69
  (12 shorter events, 0.1 us)
Async XLA Ops:
  0.6 11.8 %copy-start = (bf16[64,12,2048]{2,0,1:T(8,128)(2,1)S(1)}, bf16[64,12,2048]{2,0,1:T(8,128)(2,1)}, u32[]{:S(2)}) copy-start(bf16[64,12,2048]{2,0,1:T(8,128)(2,1)} %param.25) | copy-start | bytes 9437188
  15.9 2.0 copy-start.1
  276.9 6.2 %copy-start.8 = (bf16[2048]{0:T(1024)(128)(2,1)S(1)}, bf16[2048]{0:T(1024)(128)(2,1)}, u32[]{:S(2)}) copy-start(bf16[2048]{0:T(1024)(128)(2,1)} %param.20) | copy-start | bytes 12292
  276.9 6.2 %copy-start.3 = (bf16[64,2048]{1,0:T(8,128)(2,1)S(1)}, bf16[64,2048]{1,0:T(8,128)(2,1)}, u32[]{:S(2)}) copy-start(bf16[64,2048]{1,0:T(8,128)(2,1)} %param.19) | copy-start | bytes 786436
  276.9 8.7 %copy-start.6 = (s32[64,8]{0,1:T(8,128)S(1)}, s32[64,8]{0,1:T(8,128)}, u32[]{:S(2)}) copy-start(s32[64,8]{0,1:T(8,128)} %param.22) | copy-start | bytes 6148
  284.3 2.5 copy-start.2
  286.8 199.9 %copy-start.10 = (s32[8]{0:T(128)S(1)}, s32[8]{0:T(128)}, u32[]{:S(2)}) copy-start(s32[8]{0:T(128)} %param.18) | copy-start | bytes 100
  286.8 200.0 %copy-start.4 = (bf16[8,64,512]{2,1,0:T(8,128)(2,1)S(1)}, bf16[8,64,512]{2,1,0:T(8,128)(2,1)}, u32[]{:S(2)}) copy-start(bf16[8,64,512]{2,1,0:T(8,128)(2,1)} %param.14) | copy-start | bytes 1572868
  286.8 200.0 %copy-start.5 = (bf16[8,4096]{1,0:T(8,128)(2,1)S(1)}, bf16[8,4096]{1,0:T(8,128)(2,1)}, u32[]{:S(2)}) copy-start(bf16[8,4096]{1,0:T(8,128)(2,1)} %param.13) | copy-start | bytes 196612
  286.8 200.4 %copy-start.9 = (bf16[8,512]{1,0:T(8,128)(2,1)S(1)}, bf16[8,512]{1,0:T(8,128)(2,1)}, u32[]{:S(2)}) copy-start(bf16[8,512]{1,0:T(8,128)(2,1)} %param.16) | copy-start | bytes 24580
  286.9 200.9 %copy-start.7 = (bf16[8,512]{1,0:T(8,128)(2,1)S(1)}, bf16[8,512]{1,0:T(8,128)(2,1)}, u32[]{:S(2)}) copy-start(bf16[8,512]{1,0:T(8,128)(2,1)} %param.17) | copy-start | bytes 24580

commit v3 on v1

v3 whole, which is shorter than its diff:
```python
import functools
import math

import jax
import jax.numpy as jnp
from jax import lax
from jax.experimental import pallas as pl
from jax.experimental.pallas import tpu as pltpu
from jax.sharding import Mesh
from jax.sharding import PartitionSpec as P

HEADS = 32
KV_HEADS = 4
HEAD_DIM = 128
CTX = 64
EPSILON = 1e-06
SLOTS = 16
TEAM = 4
LANES = 128
BLOCK = 16
GU_LATE = 4
DOWN_WAIT = 3
GU_WAIT = 7

MESH = pl.DeviceIdType.MESH
EXPERT = ("z", "core")
ALL = ("team", "quad", "z", "core")


def rms_normed(hidden_in, norm_gain):
    values = hidden_in.astype(jnp.float32)
    mean_square = jnp.mean(values * values, axis=-1, keepdims=True)
    return (values * lax.rsqrt(mean_square + EPSILON) * norm_gain.astype(jnp.float32)).astype(
        jnp.bfloat16
    )


def remote(src, dst, send, recv, to):
    return pltpu.make_async_remote_copy(
        src_ref=src, dst_ref=dst, send_sem=send, recv_sem=recv, device_id=to, device_id_type=MESH
    )


def wait_bytes(ref, sem):
    pltpu.make_async_copy(ref, ref, sem).wait()


def moe_kernel(
    nz,
    x_ref,
    gain_ref,
    router_ref,
    ids_ref,
    q_ref,
    key_ref,
    value_ref,
    new_key_ref,
    new_value_ref,
    lengths_ref,
    gate_ref,
    up_ref,
    down_ref,
    o_ref,
    attended_ref,
    tokens,
    metas,
    wgu,
    down_in,
    dmat,
    gu_stage,
    down_raw,
    down_out,
    mine,
    theirs,
    outgoing,
    acc,
    picked,
    hidden,
    sels,
    upper,
    perm,
    square,
    ids_row,
    load_sem,
    raw_sem,
    own_sem,
    gu_send,
    down_send,
    gu_fwd,
    down_fwd,
    gu_recv,
    down_recv,
    gu_mate,
    down_mate,
    ring_send,
    ring_meta_send,
    pair_send,
    pair_meta_send,
    out_send,
    sum_send,
    ring_recv,
    ring_meta,
    pair_recv,
    pair_meta,
    their_recv,
    sum_recv,
):
    half_ring = nz // 2
    quad, z, core = lax.axis_index("quad"), lax.axis_index("z"), lax.axis_index("core")
    me = z * 2 + core
    rows, width = x_ref.shape
    half = rows // 2
    partner = {"core": 1 - core}
    after = {"z": lax.rem(z + 1, nz)}
    before = {"z": lax.rem(z + nz - 1, nz)}
    towards = (after, before)
    mates = [{"quad": lax.rem(quad + m, TEAM)} for m in range(1, TEAM)]
    cut = gu_stage.shape[2]
    columns = pl.ds(pl.multiple_of(quad * cut, LANES), cut)
    down_cut = width // TEAM
    down_rows = down_ref.shape[0]
    message = down_in.shape[2]
    strips = message // down_rows
    block = down_raw.shape[2]
    blocks = 2 * nz // block

    stage_from = pl.ds(pl.multiple_of(lax.rem(quad, TEAM // 2) * cut, LANES), cut)

    @pl.when(quad < TEAM // 2)
    def _():
        pltpu.make_async_copy(gate_ref.at[:, :, stage_from], gu_stage, load_sem).start()

    @pl.when(quad >= TEAM // 2)
    def _():
        pltpu.make_async_copy(up_ref.at[:, :, stage_from], gu_stage, load_sem).start()

    raw = []
    for c in range(strips):
        for g in range(blocks):
            at = pl.ds(pl.multiple_of(quad * down_cut + c * LANES, LANES), LANES)
            raw.append(
                pltpu.make_async_copy(
                    down_ref.at[:, pl.ds(g * block, block), at],
                    down_raw.at[c, :, :, pl.ds(g * LANES, LANES)],
                    raw_sem.at[c * blocks + g],
                )
            )
    for copy in raw:
        copy.start()

    barrier = pltpu.get_barrier_semaphore()

    def greet(i, carry):
        for cc in range(2):
            pl.semaphore_signal(
                barrier, inc=1, device_id={"z": lax.rem(z + i, nz), "core": cc}, device_id_type=MESH
            )
        return carry

    lax.fori_loop(1, nz, greet, 0)
    for who in [partner] + mates:
        pl.semaphore_signal(barrier, inc=1, device_id=who, device_id_type=MESH)

    across = lax.broadcasted_iota(jnp.int32, (LANES, LANES), 1)
    below = lax.broadcasted_iota(jnp.int32, (LANES, LANES), 0)
    normed = rms_normed(x_ref[...], gain_ref[...])
    tokens[z, 0] = normed
    square[...] = jnp.zeros_like(square)
    square[pl.ds(0, 2 * nz), pl.ds(0, rows)] = lax.dot_general(
        router_ref[...], normed, (((1,), (1,)), ((), ())), preferred_element_type=jnp.float32
    )
    logits = square[...]
    ids_row[...] = jnp.zeros_like(ids_row)
    ids_row[:, pl.ds(0, rows)] = ids_ref[...]
    chosen = jnp.concatenate(
        [
            jnp.sum(
                jnp.where(below == ids_row[k : k + 1, :], logits, 0.0), axis=0, keepdims=True
            )
            for k in range(ids_row.shape[0])
        ],
        axis=0,
    )
    exps = jnp.exp(chosen - jnp.max(chosen, axis=0, keepdims=True))
    mixing = exps / jnp.sum(exps, axis=0, keepdims=True)
    lane = lax.broadcasted_iota(jnp.int32, mixing.shape, 1)
    metas[z, 0] = jnp.where(
        lane < rows, ids_row[...].astype(jnp.float32), pltpu.roll(mixing, rows, 1)
    )
    upper[...] = jnp.where(
        (below < across) & ((below >= rows) == (across >= rows)), 1.0, 0.0
    ).astype(jnp.bfloat16)

    size = block * message
    target = lax.broadcasted_iota(jnp.int32, (size, size), 0)
    source = lax.broadcasted_iota(jnp.int32, (1, size), 1)
    expert_of = lax.rem(source, block)
    perm[...] = jnp.where(
        target == expert_of * message + (source - expert_of) // block, 1.0, 0.0
    ).astype(jnp.bfloat16)
    for copy in raw:
        copy.wait()
    ordered = jnp.dot(
        perm[...], down_raw[...].reshape(size, blocks * LANES), preferred_element_type=jnp.float32
    ).astype(jnp.bfloat16)
    for g in range(blocks):
        down_out[pl.ds(g * block, block)] = ordered[:, g * LANES : (g + 1) * LANES].reshape(
            block, message, LANES
        )

    source_of = source // message
    within = source - source_of * message
    strip_of = within // down_rows
    perm[...] = jnp.where(
        target
        == strip_of * (block * down_rows) + source_of * down_rows + within - strip_of * down_rows,
        1.0,
        0.0,
    ).astype(jnp.bfloat16)

    wait_bytes(gu_stage, load_sem)
    pl.semaphore_wait(barrier, 2 * (nz - 1) + 1 + TEAM - 1)

    def gu_at(index):
        return wgu.at[index, :, columns]

    def send_gu(e, ahead, to):
        remote(gu_stage.at[e], gu_at(me), gu_send, gu_recv.at[ahead], to).start()

    def send_down(e, ahead, to):
        remote(down_out.at[e], down_in.at[quad, me], down_send, down_recv.at[ahead], to).start()

    own_gu = pltpu.make_async_copy(gu_stage.at[me], gu_at(me), own_sem.at[0])
    own_down = pltpu.make_async_copy(down_out.at[me], down_in.at[quad, me], own_sem.at[1])
    own_gu.start()
    own_down.start()

    def chip_behind(way, s):
        return lax.rem(z + (nz - s if way == 0 else s), nz)

    def ring(way, s, part):
        at = tokens.at[chip_behind(way, s - 1), 0, pl.ds(part * half, half)]
        return remote(at, at, ring_send, ring_recv.at[way, s - 1, part], towards[way])

    def ring_metas(way, s):
        at = metas.at[chip_behind(way, s - 1), 0]
        return remote(at, at, ring_meta_send, ring_meta.at[way, s - 1], towards[way])

    def wait_ring(way, s, part):
        wait_bytes(
            tokens.at[chip_behind(way, s), 0, pl.ds(part * half, half)],
            ring_recv.at[way, s - 1, part],
        )

    def wait_ring_meta(way, s):
        wait_bytes(metas.at[chip_behind(way, s), 0], ring_meta.at[way, s - 1])

    def pair_up(t, way, s):
        remote(
            tokens.at[t, 0], tokens.at[t, 1], pair_send, pair_recv.at[way, s - 1], partner
        ).start()
        remote(
            metas.at[t, 0], metas.at[t, 1], pair_meta_send, pair_meta.at[way, s - 1], partner
        ).start()

    for way in range(2):
        ring_metas(way, 1).start()
        for part in range(2):
            ring(way, 1, part).start()
    pair_up(z, 1, half_ring)
    send_down(z * 2 + 1 - core, 0, partner)
    send_gu(z * 2 + 1 - core, 0, partner)

    def share_gu(zz):
        at = wgu.at[pl.ds(zz * 2, 2), :, columns]
        for m in range(1, TEAM):
            remote(at, at, gu_fwd, gu_mate.at[m - 1], mates[m - 1]).start()

    def share_down(zz):
        at = down_in.at[quad, pl.ds(zz * 2, 2)]
        for m in range(1, TEAM):
            remote(at, at, down_fwd, down_mate.at[m - 1], mates[m - 1]).start()

    own_down.wait()
    wait_bytes(down_in.at[quad, z * 2 + 1 - core], down_recv.at[0])
    share_down(z)
    own_gu.wait()
    wait_bytes(gu_at(z * 2 + 1 - core), gu_recv.at[0])
    share_gu(z)

    def both_ways(dist, act):
        act(dist)

        @pl.when(dist < half_ring)
        def _():
            act(nz - dist)

    def issue(send):
        def act(ahead):
            zz = lax.rem(z + ahead, nz)
            for cc in range(2):
                send(zz * 2 + cc, ahead, {"z": zz, "core": cc})

        return act

    def arrived_gu(ahead):
        zz = lax.rem(z - ahead + nz, nz)
        wait_bytes(wgu.at[pl.ds(zz * 2, 2), :, columns], gu_recv.at[ahead])
        share_gu(zz)

    def arrived_down(ahead):
        zz = lax.rem(z - ahead + nz, nz)
        wait_bytes(down_in.at[quad, pl.ds(zz * 2, 2)], down_recv.at[ahead])
        share_down(zz)

    def when_step(u, late, act):
        @pl.when((u > late) & (u <= half_ring + late))
        def _():
            both_ways(half_ring + 1 + late - u, act)

    def weight_step(u):
        when_step(u, 0, issue(send_down))
        when_step(u, GU_LATE, issue(send_gu))
        when_step(u, DOWN_WAIT, arrived_down)
        when_step(u, GU_WAIT, arrived_gu)

    def attend(s):
        queries, keys, values = q_ref[s], key_ref[s], value_ref[s]
        fresh_keys = new_key_ref[s].astype(jnp.float32)
        fresh_values = new_value_ref[s].astype(jnp.float32)
        group_size = HEADS // KV_HEADS
        scale = 1.0 / math.sqrt(HEAD_DIM)
        visible = lax.broadcasted_iota(jnp.int32, (group_size, CTX), 1) < lengths_ref[s]
        for g in range(KV_HEADS):
            at = slice(g * HEAD_DIM, (g + 1) * HEAD_DIM)
            query = queries[g * group_size : (g + 1) * group_size]
            scores = scale * lax.dot_general(
                query, keys[:, at], (((1,), (1,)), ((), ())), preferred_element_type=jnp.float32
            )
            own_score = scale * jnp.sum(
                query.astype(jnp.float32) * fresh_keys[:, at], axis=1, keepdims=True
            )
            scores = jnp.where(visible, scores, -1e30)
            largest = jnp.maximum(jnp.max(scores, axis=1, keepdims=True), own_score)
            cached_exp = jnp.exp(scores - largest)
            own_exp = jnp.exp(own_score - largest)
            prob_total = jnp.sum(cached_exp, axis=1, keepdims=True) + own_exp
            cached_prob = (cached_exp / prob_total).astype(jnp.bfloat16)
            own_prob = (own_exp / prob_total).astype(jnp.bfloat16).astype(jnp.float32)
            context = jnp.dot(cached_prob, values[:, at], preferred_element_type=jnp.float32)
            context = context + own_prob * fresh_values[:, at]
            attended_ref[s, pl.ds(g * group_size, group_size), :] = context.astype(jnp.bfloat16)

    def ring_step(s, carry):
        for part in range(2):
            for way in range(2):
                if part == 0:
                    wait_ring_meta(way, s)
                    ring_metas(way, s + 1).start()
                wait_ring(way, s, part)
                ring(way, s + 1, part).start()
        for way in range(2):
            pair_up(chip_behind(way, s), way, s)
        weight_step(s)

        @pl.when(s <= q_ref.shape[0])
        def _():
            attend(s - 1)

        return carry

    lax.fori_loop(1, half_ring - 1, ring_step, 0)

    s = half_ring - 1
    for way in range(2):
        wait_ring_meta(way, s)
        if way == 0:
            ring_metas(way, s + 1).start()
        wait_ring(way, s, way)
        ring(way, s + 1, way).start()
    for way in range(2):
        wait_ring(way, s, 1 - way)
        pair_up(chip_behind(way, s), way, s)

    def weights_only(u, carry):
        weight_step(u)
        return carry

    lax.fori_loop(s, s + 1, weights_only, 0)
    s = half_ring
    wait_ring_meta(0, s)
    wait_ring(0, s, 0)
    wait_ring(1, s, 1)
    far = chip_behind(0, s)
    pair_up(far, 0, s)

    lax.fori_loop(s, half_ring + DOWN_WAIT + 1, weights_only, 0)
    for m in range(1, TEAM):
        wait_bytes(down_in.at[lax.rem(quad - m + TEAM, TEAM)], down_mate.at[m - 1])
    for g in range(blocks):
        arrived = jnp.concatenate(
            [down_in[q, pl.ds(g * block, block)].reshape(size, LANES) for q in range(TEAM)], axis=1
        )
        ordered = jnp.dot(perm[...], arrived, preferred_element_type=jnp.float32).astype(
            jnp.bfloat16
        )
        span = block * down_rows
        for c in range(strips):
            for q in range(TEAM):
                dmat[pl.ds(g * span, span), pl.ds(q * down_cut + c * LANES, LANES)] = ordered[
                    c * span : (c + 1) * span, q * LANES : (q + 1) * LANES
                ]
    lax.fori_loop(half_ring + DOWN_WAIT + 1, half_ring + GU_WAIT + 1, weights_only, 0)

    expert = me.astype(jnp.float32)

    def routing(t):
        own, other = metas[t, 0], metas[t, 1]
        lane = lax.broadcasted_iota(jnp.int32, own.shape, 1)
        ids = jnp.where(lane < rows, own, pltpu.roll(other, rows, 1))
        weights = jnp.where(lane < rows, pltpu.roll(own, rows, 1), other)
        same = ids == expert
        hit = jnp.sum(jnp.where(same, 1.0, 0.0), axis=0, keepdims=True)
        mix = jnp.sum(jnp.where(same, weights, 0.0), axis=0, keepdims=True)
        hits = jnp.broadcast_to(hit, own.shape).astype(jnp.bfloat16)
        rank = jnp.dot(hits, upper[...], preferred_element_type=jnp.float32)[0:1]
        lane = lax.broadcasted_iota(jnp.int32, (2 * SLOTS, LANES), 1)
        slot = lax.broadcasted_iota(jnp.int32, (2 * SLOTS, LANES), 0)
        rank = rank + jnp.where(lane < rows, 0.0, float(SLOTS))
        sel = jnp.where((slot.astype(jnp.float32) == rank) & (hit > 0.5), 1.0, 0.0)
        return sel, jnp.sum(sel * mix, axis=1, keepdims=True)

    def chips(s):
        return (lax.rem(z - s + nz, nz), lax.rem(z + lax.rem(s, half_ring), nz))

    def gather_part(s):
        mixes = []
        for i, t in enumerate(chips(s)):
            wait_bytes(tokens.at[t, 1], pair_recv.at[i, s - 1])
            wait_bytes(metas.at[t, 1], pair_meta.at[i, s - 1])
            sel, mix = routing(t)
            sels[i] = sel
            mixes.append(mix)
            picked[pl.ds(2 * SLOTS * i, 2 * SLOTS), :] = jnp.dot(
                sel.astype(jnp.bfloat16),
                tokens[t].reshape(2 * rows, width),
                preferred_element_type=jnp.float32,
            ).astype(jnp.bfloat16)
        return jnp.concatenate(mixes, axis=0)

    def first_part(s):
        mix = gather_part(s)
        gate_up = jnp.dot(
            picked[...], wgu[...].reshape(width, -1), preferred_element_type=jnp.float32
        )
        ff = gate_up.shape[1] // 2
        gate, up = gate_up[:, :ff], gate_up[:, ff:]
        hidden[...] = (gate / (1.0 + jnp.exp(-gate)) * up * mix).astype(jnp.bfloat16)

    def second_part(s):
        spot = lax.rem(s, 2)

        @pl.when(s < half_ring - 1)
        def _():
            wait_bytes(outgoing.at[spot], out_send.at[spot])

        rows_out = jnp.dot(hidden[...], dmat[...], preferred_element_type=jnp.float32).astype(
            jnp.bfloat16
        )
        for i, t in enumerate(chips(s)):
            spread = lax.dot_general(
                sels[i].astype(jnp.bfloat16),
                rows_out[2 * SLOTS * i : 2 * SLOTS * (i + 1)],
                (((0,), (0,)), ((), ())),
                preferred_element_type=jnp.float32,
            ).astype(jnp.bfloat16)
            outgoing[spot, i] = spread[rows:]
            mine[t] = spread[:rows]
        for i, t in enumerate(chips(s)):
            remote(
                outgoing.at[spot, i],
                theirs.at[t],
                out_send.at[spot],
                their_recv.at[i, s - 1],
                partner,
            ).start()

    def tokens_at(way, d):
        return lax.rem(z + (d if way == 0 else nz - d), nz)

    def wait_their(i, s):
        wait_bytes(theirs.at[chips(s)[i]], their_recv.at[i, s - 1])

    def onward(way, j, part):
        return remote(
            acc.at[way, j, pl.ds(part * half, half)],
            acc.at[way, j + 1, pl.ds(part * half, half)],
            sum_send,
            sum_recv.at[way, j, part],
            towards[way],
        )

    def add(way, j, t, part, fresh):
        at = pl.ds(part * half, half)
        total = mine[t, at, :].astype(jnp.float32) + theirs[t, at, :].astype(jnp.float32)
        if not fresh:
            total = total + acc[way, j, at, :].astype(jnp.float32)
        acc[way, j, at, :] = total.astype(jnp.bfloat16)

    def wait_sum(way, j, part):
        wait_bytes(acc.at[way, j, pl.ds(part * half, half)], sum_recv.at[way, j - 1, part])

    for m in range(1, TEAM):
        from_mate = lax.rem(quad - m + TEAM, TEAM)
        wait_bytes(
            wgu.at[:, :, pl.ds(pl.multiple_of(from_mate * cut, LANES), cut)], gu_mate.at[m - 1]
        )

    def sums(j, carry):
        d = half_ring - j

        @pl.when(j == 0)
        def _():
            first_part(half_ring)
            second_part(half_ring)
            wait_their(0, half_ring)
            for way in range(2):
                add(way, 0, far, way, True)
            for way in range(2):
                onward(way, 0, way).start()

        @pl.when(j == 1)
        def _():
            wait_their(0, d)
            wait_their(1, d)
            for way in range(2):
                add(way, 1, tokens_at(way, d), 1 - way, True)
            for way in range(2):
                onward(way, 1, 1 - way).start()

        @pl.when(j > 1)
        def _():
            wait_their(0, d)
            wait_their(1, d)
            for way in range(2):
                wait_sum(way, j, 0)
                add(way, j, tokens_at(way, d), 0, False)
            for way in range(2):
                onward(way, j, 0).start()

        @pl.when(d > 1)
        def _():
            first_part(d - 1)

        @pl.when(j == 1)
        def _():
            for way in range(2):
                wait_sum(way, 1, way)
                add(way, 1, tokens_at(way, d), way, False)
            for way in range(2):
                onward(way, 1, way).start()

        @pl.when(j > 1)
        def _():
            for way in range(2):
                wait_sum(way, j, 1)
                add(way, j, tokens_at(way, d), 1, False)
            for way in range(2):
                onward(way, j, 1).start()

        @pl.when(d > 1)
        def _():
            second_part(d - 1)

        return carry

    lax.fori_loop(0, half_ring, sums, 0)

    wait_their(1, half_ring)
    for part in range(2):
        at = pl.ds(part * half, half)
        for way in range(2):
            wait_sum(way, half_ring, part)
        o_ref[at, :] = (
            mine[z, at, :].astype(jnp.float32)
            + theirs[z, at, :].astype(jnp.float32)
            + acc[0, half_ring, at, :].astype(jnp.float32)
            + acc[1, half_ring, at, :].astype(jnp.float32)
        ).astype(jnp.bfloat16)

    wait_bytes(gu_stage.at[pl.ds(0, 2 * nz - 1)], gu_send)
    wait_bytes(down_out.at[pl.ds(0, 2 * nz - 1)], down_send)
    wait_bytes(wgu.at[:, :, pl.ds(0, (TEAM - 1) * cut)], gu_fwd)
    wait_bytes(down_in.at[pl.ds(0, TEAM - 1)], down_fwd)
    wait_bytes(mine.at[pl.ds(0, nz - 1)], ring_send)
    wait_bytes(metas.at[pl.ds(0, nz - 1), 0], ring_meta_send)
    wait_bytes(mine, pair_send)
    wait_bytes(metas.at[:, 0], pair_meta_send)
    wait_bytes(mine.at[pl.ds(0, nz - 1)], sum_send)
    wait_bytes(outgoing.at[0], out_send.at[0])
    wait_bytes(outgoing.at[1], out_send.at[1])


def moe(hidden_in, gain, router, ids, attention, gate, up, down, nz):
    rows, width = hidden_in.shape
    ff = gate.shape[2]
    top_count = ids.shape[0]
    down_rows = down.shape[0]
    message = down_rows * width // TEAM // LANES
    bf16 = jnp.bfloat16
    steps = nz // 2
    vmem = pltpu.VMEM
    dma = pltpu.SemaphoreType.DMA
    strips = message // down_rows
    blocks = 2 * nz // BLOCK
    here = pl.BlockSpec(memory_space=vmem)
    return pl.pallas_call(
        functools.partial(moe_kernel, nz),
        name="moe",
        out_shape=(
            jax.ShapeDtypeStruct((rows, width), bf16),
            jax.ShapeDtypeStruct(attention[0].shape, bf16),
        ),
        in_specs=[here] * 9
        + [pl.BlockSpec(memory_space=pltpu.SMEM)]
        + [pl.BlockSpec(memory_space=pl.ANY)] * 3,
        out_specs=(here, here),
        scratch_shapes=[
            vmem((nz, 2, rows, width), bf16),
            vmem((nz, 2, 8, LANES), jnp.float32),
            vmem((2 * nz, gate.shape[1], 2 * ff), bf16),
            vmem((TEAM, 2 * nz, message, LANES), bf16),
            vmem((ff, width), bf16),
            vmem((2 * nz, gate.shape[1], 2 * ff // TEAM), bf16),
            vmem((strips, down_rows, BLOCK, blocks * LANES), bf16),
            vmem((2 * nz, message, LANES), bf16),
            vmem((nz, rows, width), bf16),
            vmem((nz, rows, width), bf16),
            vmem((2, 2, rows, width), bf16),
            vmem((2, steps + 1, rows, width), bf16),
            vmem((4 * SLOTS, width), bf16),
            vmem((4 * SLOTS, ff), bf16),
            vmem((2, 2 * SLOTS, LANES), jnp.float32),
            vmem((LANES, LANES), bf16),
            vmem((BLOCK * message, BLOCK * message), bf16),
            vmem((LANES, LANES), jnp.float32),
            vmem((top_count, LANES), jnp.int32),
            dma,
            dma((strips * blocks,)),
            dma((2,)),
            dma,
            dma,
            dma,
            dma,
            dma((nz,)),
            dma((nz,)),
            dma((TEAM - 1,)),
            dma((TEAM - 1,)),
            dma,
            dma,
            dma,
            dma,
            dma((2,)),
            dma,
            dma((2, steps, 2)),
            dma((2, steps)),
            dma((2, steps)),
            dma((2, steps)),
            dma((2, steps)),
            dma((2, steps, 2)),
        ],
        compiler_params=pltpu.CompilerParams(
            collective_id=0, has_side_effects=True, vmem_limit_bytes=63 << 20
        ),
    )(hidden_in, gain, router, ids, *attention, gate, up, down)


def local(
    nz,
    queries,
    key_cache,
    value_cache,
    new_key,
    new_value,
    cache_lengths,
    hidden_in,
    norm_gain,
    router_weight,
    expert_ids,
    gate_train,
    up_train,
    down_train,
):
    seq_count = queries.shape[0]
    attention = (
        queries.reshape(seq_count, HEADS, HEAD_DIM),
        key_cache,
        value_cache,
        new_key[:, None, :],
        new_value[:, None, :],
        cache_lengths,
    )
    mixed, attended = moe(
        hidden_in,
        norm_gain[None, :],
        router_weight.T,
        expert_ids.T,
        attention,
        gate_train,
        up_train,
        jnp.swapaxes(down_train, 0, 1),
        nz,
    )
    return attended.reshape(seq_count, HEADS * HEAD_DIM), mixed


def solution(mesh):
    groups, nz = mesh.shape["groups"], mesh.shape["expert"] // 2
    torus = Mesh(mesh.devices.reshape(groups // TEAM, TEAM, nz, 2), ALL)
    placed = (
        P(ALL, None),
        P(ALL, None, None),
        P(ALL, None, None),
        P(ALL, None),
        P(ALL, None),
        P(ALL),
        P(ALL, None),
        P(),
        P(),
        P(ALL, None),
        P(None, EXPERT, None),
        P(None, EXPERT, None),
        P(None, EXPERT, None),
    )
    return jax.shard_map(
        functools.partial(local, nz),
        mesh=torus,
        in_specs=placed,
        out_specs=(P(ALL, None), P(ALL, None)),
        check_vma=False,
    )
```

time: 496 us -> 460 us (0.927)
  local copies, waits for them, and re-layouts: 29.1 us -> 8.55 us
  other arithmetic: 7.78 us -> 0 us
    reshape x4 -> x0, local copies, waits for them, and re-layouts: 14.3 us -> none  [the longest x2 7.57 us: pack(): a.reshape(count, a.shape[1], -1, LANES)]
    transpose x3 -> x0, local copies, waits for them, and re-layouts: 8.61 us -> none  [the longest x2 4.51 us: pack(): jnp.swapaxes(a.reshape(count, a.shape[1], -1, LANES), 1, 2)]
    pallas_call x2 -> x1, Pallas kernels: 454 us -> 450 us  [moe(): pl.pallas_call(functools.partial(moe_kernel, nz), name='moe', out_shape=(...]
where the time goes in v3:
time: 460 us; the launch traced here: 459 us
  Pallas kernels  450 us (98%)
  local copies, waits for them, and re-layouts  8.55 us (2%)
    pallas_call x1, Pallas kernels, moe(): pl.pallas_call(functools.partial(moe_kernel, nz), name='moe', out_shape=(...  450 us

profile of v3, /device:TPU:38, one launch (start us, length us, event | category | flops | bytes accessed | tf_op | source)
XLA Modules:
  0.0 459.3 jit_solution(3824310776617343952)
XLA Ops:
  0.6 1.3 broadcast_in_dim.9.gain_ref
  1.9 1.3 copy.15.new_key_ref
  3.2 1.3 copy.16.new_value_ref
  4.5 1.5 copy.22
  6.0 450.1 %moe.1 = (bf16[64,2048]{1,0:T(8,128)(2,1)}, bf16[8,32,128]{2,1,0:T(8,128)(2,1)}) custom-call(bf16[64,2048]{1,0:T(8,128)(2,1)} %x_ref.1, bf16[1,2048]{1,0:T(2,128)(2,1)} %broadcast_in_dim.9.gain_ref, bf16[64,2048]{1,0:T(8,128)(2,1)} %bitcast.15, s32[8,64]{1,0:T(8,128)} %bitcast.21, bf16[8,32,128]{2,1,0:T(8,128)(2,1)} %bitcast.14, ...), custom_call_target="tpu_custom_call" | custom-call | tf_op jit(solution)/shard_map/moe/pallas_call | solution.py:617
  456.1 1.5 copy.21
  457.6 1.7 copy.24

commit v4 on v3

--- a/solution.py
+++ b/solution.py
@@ -18,9 +18,8 @@
 TEAM = 4
 LANES = 128
 BLOCK = 16
-GU_LATE = 4
-DOWN_WAIT = 3
-GU_WAIT = 7
+TAIL = 4
+EARLY = 8
 
 MESH = pl.DeviceIdType.MESH
 EXPERT = ("z", "core")
@@ -263,11 +262,6 @@
             metas.at[t, 0], metas.at[t, 1], pair_meta_send, pair_meta.at[way, s - 1], partner
         ).start()
 
-    for way in range(2):
-        ring_metas(way, 1).start()
-        for part in range(2):
-            ring(way, 1, part).start()
-    pair_up(z, 1, half_ring)
     send_down(z * 2 + 1 - core, 0, partner)
     send_gu(z * 2 + 1 - core, 0, partner)
 
@@ -313,16 +307,20 @@
         wait_bytes(down_in.at[quad, pl.ds(zz * 2, 2)], down_recv.at[ahead])
         share_down(zz)
 
-    def when_step(u, late, act):
-        @pl.when((u > late) & (u <= half_ring + late))
-        def _():
-            both_ways(half_ring + 1 + late - u, act)
-
-    def weight_step(u):
-        when_step(u, 0, issue(send_down))
-        when_step(u, GU_LATE, issue(send_gu))
-        when_step(u, DOWN_WAIT, arrived_down)
-        when_step(u, GU_WAIT, arrived_gu)
+    def over_distances(first, last, act):
+        def body(dist, carry):
+            both_ways(dist, act)
+            return carry
+
+        lax.fori_loop(first, last + 1, body, 0)
+
+    over_distances(1, half_ring, issue(send_down))
+    over_distances(1, half_ring, issue(send_gu))
+    for way in range(2):
+        ring_metas(way, 1).start()
+        for part in range(2):
+            ring(way, 1, part).start()
+    pair_up(z, 1, half_ring)
 
     def attend(s):
         queries, keys, values = q_ref[s], key_ref[s], value_ref[s]
@@ -351,50 +349,14 @@
             context = context + own_prob * fresh_values[:, at]
             attended_ref[s, pl.ds(g * group_size, group_size), :] = context.astype(jnp.bfloat16)
 
-    def ring_step(s, carry):
-        for part in range(2):
-            for way in range(2):
-                if part == 0:
-                    wait_ring_meta(way, s)
-                    ring_metas(way, s + 1).start()
-                wait_ring(way, s, part)
-                ring(way, s + 1, part).start()
-        for way in range(2):
-            pair_up(chip_behind(way, s), way, s)
-        weight_step(s)
-
-        @pl.when(s <= q_ref.shape[0])
-        def _():
-            attend(s - 1)
-
+    over_distances(1, half_ring, arrived_down)
+    over_distances(1, half_ring // 2, arrived_gu)
+
+    def attend_one(s, carry):
+        attend(s)
         return carry
 
-    lax.fori_loop(1, half_ring - 1, ring_step, 0)
-
-    s = half_ring - 1
-    for way in range(2):
-        wait_ring_meta(way, s)
-        if way == 0:
-            ring_metas(way, s + 1).start()
-        wait_ring(way, s, way)
-        ring(way, s + 1, way).start()
-    for way in range(2):
-        wait_ring(way, s, 1 - way)
-        pair_up(chip_behind(way, s), way, s)
-
-    def weights_only(u, carry):
-        weight_step(u)
-        return carry
-
-    lax.fori_loop(s, s + 1, weights_only, 0)
-    s = half_ring
-    wait_ring_meta(0, s)
-    wait_ring(0, s, 0)
-    wait_ring(1, s, 1)
-    far = chip_behind(0, s)
-    pair_up(far, 0, s)
-
-    lax.fori_loop(s, half_ring + DOWN_WAIT + 1, weights_only, 0)
+    lax.fori_loop(0, q_ref.shape[0], attend_one, 0)
     for m in range(1, TEAM):
         wait_bytes(down_in.at[lax.rem(quad - m + TEAM, TEAM)], down_mate.at[m - 1])
     for g in range(blocks):
@@ -410,8 +372,7 @@
                 dmat[pl.ds(g * span, span), pl.ds(q * down_cut + c * LANES, LANES)] = ordered[
                     c * span : (c + 1) * span, q * LANES : (q + 1) * LANES
                 ]
-    lax.fori_loop(half_ring + DOWN_WAIT + 1, half_ring + GU_WAIT + 1, weights_only, 0)
-
+    over_distances(half_ring // 2 + 1, half_ring - TAIL, arrived_gu)
     expert = me.astype(jnp.float32)
 
     def routing(t):
@@ -460,7 +421,7 @@
     def second_part(s):
         spot = lax.rem(s, 2)
 
-        @pl.when(s < half_ring - 1)
+        @pl.when(s > 2)
         def _():
             wait_bytes(outgoing.at[spot], out_send.at[spot])
 
@@ -510,11 +471,62 @@
     def wait_sum(way, j, part):
         wait_bytes(acc.at[way, j, pl.ds(part * half, half)], sum_recv.at[way, j - 1, part])
 
-    for m in range(1, TEAM):
-        from_mate = lax.rem(quad - m + TEAM, TEAM)
-        wait_bytes(
-            wgu.at[:, :, pl.ds(pl.multiple_of(from_mate * cut, LANES), cut)], gu_mate.at[m - 1]
-        )
+    def ring_step(s, carry):
+        chunk = s - (half_ring - 2 - EARLY)
+        for part in range(2):
+            for way in range(2):
+                if part == 0:
+                    wait_ring_meta(way, s)
+                    ring_metas(way, s + 1).start()
+                wait_ring(way, s, part)
+                ring(way, s + 1, part).start()
+            if part == 0:
+
+                @pl.when(chunk > 0)
+                def _():
+                    first_part(chunk)
+
+        for way in range(2):
+            pair_up(chip_behind(way, s), way, s)
+
+        @pl.when(chunk > 0)
+        def _():
+            second_part(chunk)
+
+        @pl.when(s <= TAIL)
+        def _():
+            both_ways(half_ring - TAIL + s, arrived_gu)
+
+        @pl.when(s == TAIL + 2)
+        def _():
+            for m in range(1, TEAM):
+                from_mate = lax.rem(quad - m + TEAM, TEAM)
+                wait_bytes(
+                    wgu.at[:, :, pl.ds(pl.multiple_of(from_mate * cut, LANES), cut)],
+                    gu_mate.at[m - 1],
+                )
+
+        return carry
+
+    lax.fori_loop(1, half_ring - 1, ring_step, 0)
+
+    s = half_ring - 1
+    for way in range(2):
+        wait_ring_meta(way, s)
+        if way == 0:
+            ring_metas(way, s + 1).start()
+        wait_ring(way, s, way)
+        ring(way, s + 1, way).start()
+    for way in range(2):
+        wait_ring(way, s, 1 - way)
+        pair_up(chip_behind(way, s), way, s)
+
+    s = half_ring
+    wait_ring_meta(0, s)
+    wait_ring(0, s, 0)
+    wait_ring(1, s, 1)
+    far = chip_behind(0, s)
+    pair_up(far, 0, s)
 
     def sums(j, carry):
         d = half_ring - j
@@ -548,7 +560,7 @@
             for way in range(2):
                 onward(way, j, 0).start()
 
-        @pl.when(d > 1)
+        @pl.when(d > EARLY + 1)
         def _():
             first_part(d - 1)
 
@@ -568,7 +580,7 @@
             for way in range(2):
                 onward(way, j, 1).start()
 
-        @pl.when(d > 1)
+        @pl.when(d > EARLY + 1)
         def _():
             second_part(d - 1)
 

time: 460 us -> 443 us (0.963)
  Pallas kernels: 450 us -> 433 us
    pallas_call x1, Pallas kernels: 450 us -> 433 us  [moe(): pl.pallas_call(functools.partial(moe_kernel, nz), name='moe', out_shape=(...]
where the time goes in v4:
time: 443 us; the launch traced here: 442 us
  Pallas kernels  433 us (98%)
  local copies, waits for them, and re-layouts  8.55 us (2%)
    pallas_call x1, Pallas kernels, moe(): pl.pallas_call(functools.partial(moe_kernel, nz), name='moe', out_shape=(...  433 us

profile of v4, /device:TPU:38, one launch (start us, length us, event | category | flops | bytes accessed | tf_op | source)
XLA Modules:
  0.0 442.2 jit_solution(1197920177646415668)
XLA Ops:
  0.6 1.3 broadcast_in_dim.9.gain_ref
  1.9 1.3 copy.15.new_key_ref
  3.2 1.3 copy.16.new_value_ref
  4.5 1.5 copy.22
  6.0 433.0 %moe.1 = (bf16[64,2048]{1,0:T(8,128)(2,1)}, bf16[8,32,128]{2,1,0:T(8,128)(2,1)}) custom-call(bf16[64,2048]{1,0:T(8,128)(2,1)} %x_ref.1, bf16[1,2048]{1,0:T(2,128)(2,1)} %broadcast_in_dim.9.gain_ref, bf16[64,2048]{1,0:T(8,128)(2,1)} %bitcast.15, s32[8,64]{1,0:T(8,128)} %bitcast.21, bf16[8,32,128]{2,1,0:T(8,128)(2,1)} %bitcast.14, ...), custom_call_target="tpu_custom_call" | custom-call | tf_op jit(solution)/shard_map/moe/pallas_call | solution.py:629
  439.0 1.5 copy.21
  440.5 1.7 copy.24

commit v5 on v4

--- a/solution.py
+++ b/solution.py
@@ -20,6 +20,7 @@
 BLOCK = 16
 TAIL = 4
 EARLY = 8
+PIECES = 4
 
 MESH = pl.DeviceIdType.MESH
 EXPERT = ("z", "core")
@@ -108,7 +109,8 @@
     quad, z, core = lax.axis_index("quad"), lax.axis_index("z"), lax.axis_index("core")
     me = z * 2 + core
     rows, width = x_ref.shape
-    half = rows // 2
+    piece = rows // PIECES
+    halves = (range(PIECES // 2), range(PIECES // 2, PIECES))
     partner = {"core": 1 - core}
     after = {"z": lax.rem(z + 1, nz)}
     before = {"z": lax.rem(z + nz - 1, nz)}
@@ -238,7 +240,7 @@
         return lax.rem(z + (nz - s if way == 0 else s), nz)
 
     def ring(way, s, part):
-        at = tokens.at[chip_behind(way, s - 1), 0, pl.ds(part * half, half)]
+        at = tokens.at[chip_behind(way, s - 1), 0, pl.ds(part * piece, piece)]
         return remote(at, at, ring_send, ring_recv.at[way, s - 1, part], towards[way])
 
     def ring_metas(way, s):
@@ -247,7 +249,7 @@
 
     def wait_ring(way, s, part):
         wait_bytes(
-            tokens.at[chip_behind(way, s), 0, pl.ds(part * half, half)],
+            tokens.at[chip_behind(way, s), 0, pl.ds(part * piece, piece)],
             ring_recv.at[way, s - 1, part],
         )
 
@@ -318,7 +320,7 @@
     over_distances(1, half_ring, issue(send_gu))
     for way in range(2):
         ring_metas(way, 1).start()
-        for part in range(2):
+        for part in range(PIECES):
             ring(way, 1, part).start()
     pair_up(z, 1, half_ring)
 
@@ -454,33 +456,33 @@
 
     def onward(way, j, part):
         return remote(
-            acc.at[way, j, pl.ds(part * half, half)],
-            acc.at[way, j + 1, pl.ds(part * half, half)],
+            acc.at[way, j, pl.ds(part * piece, piece)],
+            acc.at[way, j + 1, pl.ds(part * piece, piece)],
             sum_send,
             sum_recv.at[way, j, part],
             towards[way],
         )
 
     def add(way, j, t, part, fresh):
-        at = pl.ds(part * half, half)
+        at = pl.ds(part * piece, piece)
         total = mine[t, at, :].astype(jnp.float32) + theirs[t, at, :].astype(jnp.float32)
         if not fresh:
             total = total + acc[way, j, at, :].astype(jnp.float32)
         acc[way, j, at, :] = total.astype(jnp.bfloat16)
 
     def wait_sum(way, j, part):
-        wait_bytes(acc.at[way, j, pl.ds(part * half, half)], sum_recv.at[way, j - 1, part])
+        wait_bytes(acc.at[way, j, pl.ds(part * piece, piece)], sum_recv.at[way, j - 1, part])
 
     def ring_step(s, carry):
         chunk = s - (half_ring - 2 - EARLY)
-        for part in range(2):
+        for part in range(PIECES):
             for way in range(2):
                 if part == 0:
                     wait_ring_meta(way, s)
                     ring_metas(way, s + 1).start()
                 wait_ring(way, s, part)
                 ring(way, s + 1, part).start()
-            if part == 0:
+            if part == PIECES // 2 - 1:
 
                 @pl.when(chunk > 0)
                 def _():
@@ -515,16 +517,19 @@
         wait_ring_meta(way, s)
         if way == 0:
             ring_metas(way, s + 1).start()
-        wait_ring(way, s, way)
-        ring(way, s + 1, way).start()
+        for part in halves[way]:
+            wait_ring(way, s, part)
+            ring(way, s + 1, part).start()
     for way in range(2):
-        wait_ring(way, s, 1 - way)
+        for part in halves[1 - way]:
+            wait_ring(way, s, part)
         pair_up(chip_behind(way, s), way, s)
 
     s = half_ring
     wait_ring_meta(0, s)
-    wait_ring(0, s, 0)
-    wait_ring(1, s, 1)
+    for way in range(2):
+        for part in halves[way]:
+            wait_ring(way, s, part)
     far = chip_behind(0, s)
     pair_up(far, 0, s)
 
@@ -536,29 +541,36 @@
             first_part(half_ring)
             second_part(half_ring)
             wait_their(0, half_ring)
-            for way in range(2):
-                add(way, 0, far, way, True)
-            for way in range(2):
-                onward(way, 0, way).start()
-
-        @pl.when(j == 1)
+            for k in range(PIECES // 2):
+                for way in range(2):
+                    add(way, 0, far, halves[way][k], True)
+                for way in range(2):
+                    onward(way, 0, halves[way][k]).start()
+
+        @pl.when(j > 0)
         def _():
             wait_their(0, d)
             wait_their(1, d)
+
+        def received(part_of):
             for way in range(2):
-                add(way, 1, tokens_at(way, d), 1 - way, True)
+                wait_sum(way, j, part_of[way])
+                add(way, j, tokens_at(way, d), part_of[way], False)
             for way in range(2):
-                onward(way, 1, 1 - way).start()
+                onward(way, j, part_of[way]).start()
+
+        @pl.when(j == 1)
+        def _():
+            for k in range(PIECES // 2):
+                for way in range(2):
+                    add(way, 1, tokens_at(way, d), halves[1 - way][k], True)
+                for way in range(2):
+                    onward(way, 1, halves[1 - way][k]).start()
 
         @pl.when(j > 1)
         def _():
-            wait_their(0, d)
-            wait_their(1, d)
-            for way in range(2):
-                wait_sum(way, j, 0)
-                add(way, j, tokens_at(way, d), 0, False)
-            for way in range(2):
-                onward(way, j, 0).start()
+            for part in halves[0]:
+                received((part, part))
 
         @pl.when(d > EARLY + 1)
         def _():
@@ -566,19 +578,13 @@
 
         @pl.when(j == 1)
         def _():
-            for way in range(2):
-                wait_sum(way, 1, way)
-                add(way, 1, tokens_at(way, d), way, False)
-            for way in range(2):
-                onward(way, 1, way).start()
+            for k in range(PIECES // 2):
+                received((halves[0][k], halves[1][k]))
 
         @pl.when(j > 1)
         def _():
-            for way in range(2):
-                wait_sum(way, j, 1)
-                add(way, j, tokens_at(way, d), 1, False)
-            for way in range(2):
-                onward(way, j, 1).start()
+            for part in halves[1]:
+                received((part, part))
 
         @pl.when(d > EARLY + 1)
         def _():
@@ -589,8 +595,8 @@
     lax.fori_loop(0, half_ring, sums, 0)
 
     wait_their(1, half_ring)
-    for part in range(2):
-        at = pl.ds(part * half, half)
+    for part in range(PIECES):
+        at = pl.ds(part * piece, piece)
         for way in range(2):
             wait_sum(way, half_ring, part)
         o_ref[at, :] = (
@@ -674,12 +680,12 @@
             dma,
             dma((2,)),
             dma,
-            dma((2, steps, 2)),
+            dma((2, steps, PIECES)),
             dma((2, steps)),
             dma((2, steps)),
             dma((2, steps)),
             dma((2, steps)),
-            dma((2, steps, 2)),
+            dma((2, steps, PIECES)),
         ],
         compiler_params=pltpu.CompilerParams(
             collective_id=0, has_side_effects=True, vmem_limit_bytes=63 << 20

time: 443 us -> 442 us (level)
  no operation moved by 1% of the time
where the time goes in v5:
time: 442 us; the launch traced here: 440 us
  Pallas kernels  431 us (98%)
  local copies, waits for them, and re-layouts  8.55 us (2%)
    pallas_call x1, Pallas kernels, moe(): pl.pallas_call(functools.partial(moe_kernel, nz), name='moe', out_shape=(...  431 us

profile of v5, /device:TPU:38, one launch (start us, length us, event | category | flops | bytes accessed | tf_op | source)
XLA Modules:
  0.0 440.3 jit_solution(18446665756423704535)
XLA Ops:
  0.6 1.3 broadcast_in_dim.9.gain_ref
  1.9 1.3 copy.15.new_key_ref
  3.2 1.3 copy.16.new_value_ref
  4.5 1.5 copy.22
  6.0 431.2 %moe.1 = (bf16[64,2048]{1,0:T(8,128)(2,1)}, bf16[8,32,128]{2,1,0:T(8,128)(2,1)}) custom-call(bf16[64,2048]{1,0:T(8,128)(2,1)} %x_ref.1, bf16[1,2048]{1,0:T(2,128)(2,1)} %broadcast_in_dim.9.gain_ref, bf16[64,2048]{1,0:T(8,128)(2,1)} %bitcast.15, s32[8,64]{1,0:T(8,128)} %bitcast.21, bf16[8,32,128]{2,1,0:T(8,128)(2,1)} %bitcast.14, ...), custom_call_target="tpu_custom_call" | custom-call | tf_op jit(solution)/shard_map/moe/pallas_call | solution.py:635
  437.2 1.5 copy.21
  438.7 1.7 copy.24
